TPU v7x, 256 devices: a whole 4x4x8 slice. The times are simulated.
256 devices in a mesh: gx: 16 (over z_hi, y), gy: 16 (over z_lo, x, core).
Axes of the slice: x: 4, y: 4, z: 8 (z_hi: 4, z_lo: 2; z = z_hi * 2 + z_lo), core: 2. Of those that a mesh axis runs over, the one named last changes fastest.
Arguments:
- goal_embed: bfloat16 [32768, 128], P(('gx', 'gy')), may hold values from -6 to 6
- goal_bins: int32 [32768], P(('gx', 'gy')), may hold values from 0 to 16383, as said below
- goal_weights: float32 [32768], P(('gx', 'gy')), may hold values from 0.1 to 10
Outputs:
- bin_mean: float32 [16384, 128], P(('gx', 'gy'))
- rarity: float32 [16384], P(('gx', 'gy'))
Inputs may be any that keep to these rules, and one draw needn't show every extreme that they name: `goal_bins`: bin b belongs to owner b // 64, owners numbered in the order of gx then gy. Of the goals of one device, at most 2 fall in the bins of one owner; some owner receives exactly 2 goals from every device.
All inputs are finite; a program needn't handle non-finite values.
Results may differ from a plain program's by a relative error of at most 0.0029.
Values may be sent and summed in bfloat16 or wider, within the bound.
A program may use at most 64 MiB of HBM per device.

v0:
```python
import jax
import jax.numpy as jnp
from jax import lax
from jax.sharding import Mesh
from jax.sharding import PartitionSpec as P

BINS_DEV = 64
GX = ("gx_0", "gx_1")
GY = ("gy_0", "gy_1", "gy_2")
GX_GY = ("gx_0", "gx_1", "gy_0", "gy_1", "gy_2")


def cut_along(array, dim, devices):
    shape = array.shape
    tiles = array.reshape(*shape[:dim], devices, shape[dim] // devices, *shape[dim + 1 :])
    return jnp.moveaxis(tiles, dim, 0)


def joined_along(tiles, dim):
    shape = list(tiles.shape[1:])
    shape[dim] *= tiles.shape[0]
    return jnp.moveaxis(tiles, 0, dim).reshape(shape)


def exchange_both(array, axis, axes, splits, concats):
    sizes = [lax.axis_size(a) for a in axes]
    tiles = cut_along(array, splits[0], sizes[0])
    tiles = jnp.moveaxis(cut_along(tiles, splits[1] + 1, sizes[1]), 0, 1)
    inside = tiles.shape[2:]
    tiles = tiles.reshape(-1, *inside)
    tiles = lax.all_to_all(tiles, axis, split_axis=0, concat_axis=0, tiled=True)
    tiles = joined_along(tiles.reshape(*sizes, *inside), concats[0] + 1)
    return joined_along(tiles, concats[1])


def over_axes(array, axes):
    for axis in axes:
        array = lax.psum(array, axis)
    return array


def shards(goal_embed, goal_bins, goal_weights):
    scaled = (goal_weights[:, None] * goal_embed.astype(jnp.float32)).astype(jnp.bfloat16)
    width = goal_embed.shape[1]
    local_goals = goal_embed.shape[0]
    across = lax.axis_size(GX)
    along = lax.axis_size(GY)
    devices = across * along
    capacity = max(2, 2 * local_goals // devices)
    owners = goal_bins // BINS_DEV
    offsets = goal_bins - owners * BINS_DEV
    member = (owners[:, None] == jnp.arange(devices, dtype=jnp.int32)[None, :]).astype(jnp.int32)
    before = jnp.cumsum(member, axis=0) - member
    places = jnp.sum(before * member, axis=1)
    slots = owners * capacity + places
    outgoing = jnp.zeros((devices * capacity, width), jnp.bfloat16).at[slots].set(scaled)
    tagging = jnp.zeros((2, devices * capacity), jnp.float32)
    tagging = tagging.at[0, slots].set(goal_weights).at[1, slots].set(offsets.astype(jnp.float32))
    outgoing = outgoing.reshape(across, along, capacity, width)
    tagging = tagging.reshape(2, across, along, capacity)
    arrived = exchange_both(outgoing, GX_GY, (GX, GY), (0, 1), (0, 1))
    tag_rows = exchange_both(tagging, GX_GY, (GX, GY), (1, 2), (1, 2))
    arrived = arrived.reshape(devices * capacity, width)
    tag_rows = tag_rows.reshape(2, devices * capacity)
    labels = lax.broadcasted_iota(jnp.int32, (BINS_DEV, 1), 0).astype(jnp.float32)
    selector = tag_rows[1][None, :] == labels
    bin_sums = jnp.dot(selector.astype(jnp.bfloat16), arrived, preferred_element_type=jnp.float32)
    bin_mass = jnp.dot(selector.astype(jnp.float32), tag_rows[0], precision=lax.Precision.HIGHEST)
    total_mass = over_axes(jnp.sum(bin_mass), GX_GY)
    bin_mean = bin_sums / (bin_mass[:, None] + 1.0)
    rarity = jnp.log(total_mass / (BINS_DEV * devices)) - jnp.log(bin_mass + 1.0)
    return (bin_mean, rarity)


def solution(mesh):
    split = Mesh(mesh.devices.reshape(4, 4, 2, 4, 2), ("gx_0", "gx_1", "gy_0", "gy_1", "gy_2"))
    placed = (P(GX_GY, None), P(GX_GY), P(GX_GY))
    return jax.shard_map(
        shards, mesh=split, in_specs=placed, out_specs=(P(GX_GY, None), P(GX_GY)), check_vma=False
    )
```

profile of v0, /device:TPU:1, one launch (start us, length us, event | category | flops | bytes accessed | tf_op | source)
XLA Modules:
  0.0 103.0 jit_solution(12554257483131188271)
XLA Ops:
  0.6 0.7 subtract_convert_fusion
  1.3 0.1 fusion.2
  1.4 0.2 reduce_window_sum.11
  1.6 0.2 select_reduce_fusion
  1.8 0.0 copy-start.1
  1.8 0.6 copy-done.1
  2.4 6.8 %scatter_fusion = f32[2,512]{1,0:T(2,128)S(1)} fusion(f32[2,512]{1,0:T(2,128)S(1)} %broadcast_in_dim.6, s32[128]{0:T(128)S(1)} %select_bitcast_fusion.1, f32[128]{0:T(128)S(1)} %copy-done.1), kind=kCustom, calls=%fused_computation | custom fusion | bytes 2560 | tf_op jit(solution)/shard_map/scatter | solution.py:58
  9.3 6.8 %scatter_fusion.1 = f32[2,512]{1,0:T(2,128)S(1)} fusion(f32[2,512]{1,0:T(2,128)S(1)} %scatter_fusion, s32[128]{0:T(128)S(1)} %get-tuple-element.4, f32[128]{0:T(128)S(1)} %get-tuple-element.2), kind=kCustom, calls=%fused_computation.1 | custom fusion | bytes 2560 | tf_op jit(solution)/shard_map/scatter | solution.py:58
  16.1 0.2 reshape_reshape.7
  16.3 0.9 copy.5
  17.2 15.6 %all-to-all-start = ((f32[256,2,1,1,2]{4,1,3,2,0:T(2,128)}), f32[256,2,1,1,2]{4,1,3,2,0:T(2,128)S(1)}, u32[]{:S(2)}, u32[]{:S(2)}) async-start(f32[256,2,1,1,2]{4,1,3,2,0:T(2,128)} %copy.5), calls=%async_computation | async-start | bytes 524288 | tf_op jit(solution)/shard_map/all_to_all | solution.py:31
  32.9 1.6 %scatter_custom_fusion.2 = bf16[512,128]{1,0:T(8,128)(2,1)} fusion(s32[128]{0:T(128)S(1)} %get-tuple-element.5, bf16[]{:T(256)} %constant.38.clone.1, bf16[128,128]{1,0:T(8,128)(2,1)S(1)} %copy-done, f32[128]{0:T(128)S(1)} %copy-done.1), kind=kCustom, calls=%fused_computation.12 | custom fusion | flops 49152 | bytes 164354 | tf_op jit(solution)/shard_map/scatter | solution.py:56
  34.5 13.8 %all-to-all-done = f32[256,2,1,1,2]{4,1,3,2,0:T(2,128)S(1)} async-done(((f32[256,2,1,1,2]{4,1,3,2,0:T(2,128)}), f32[256,2,1,1,2]{4,1,3,2,0:T(2,128)S(1)}, u32[]{:S(2)}, u32[]{:S(2)}) %all-to-all-start) | async-done | bytes 4128 | tf_op jit(solution)/shard_map/all_to_all | solution.py:31
  48.3 5.9 %all-to-all-start.1 = ((bf16[256,1,1,2,128]{4,3,2,1,0:T(2,128)(2,1)}), bf16[256,1,1,2,128]{4,3,2,1,0:T(2,128)(2,1)S(1)}, u32[]{:S(2)}, u32[]{:S(2)}) async-start(bf16[256,1,1,2,128]{4,3,2,1,0:T(2,128)(2,1)} %bitcast.12), calls=%async_computation.1 | async-start | bytes 262144 | tf_op jit(solution)/shard_map/all_to_all | solution.py:31
  54.2 0.1 eq.31
  54.4 0.1 reshape.62
  54.5 0.8 fusion.11
  55.4 12.9 %psum.35 = f32[]{:T(128)} all-reduce(f32[]{:T(128)} %get-tuple-element.10), channel_id=1, replica_groups=mesh['gx_0'=4,'gx_1'=4,'gy_0'=2,'gy_1'=4,'gy_2'=2] {'gx_0'}, use_global_device_ids=true, to_apply=%region_6.7 | all-reduce | flops 1 | bytes 8 | tf_op jit(solution)/shard_map/psum | solution.py:38
  68.2 8.9 %psum.36 = f32[]{:T(128)} all-reduce(f32[]{:T(128)} %psum.35), channel_id=1, replica_groups=mesh['gx_0'=4,'gx_1'=4,'gy_0'=2,'gy_1'=4,'gy_2'=2] {'gx_1'}, use_global_device_ids=true, to_apply=%region_7.8 | all-reduce | flops 1 | bytes 8 | tf_op jit(solution)/shard_map/psum | solution.py:38
  77.1 4.4 %psum.37 = f32[]{:T(128)} all-reduce(f32[]{:T(128)} %psum.36), channel_id=1, replica_groups=mesh['gx_0'=4,'gx_1'=4,'gy_0'=2,'gy_1'=4,'gy_2'=2] {'gy_0'}, use_global_device_ids=true, to_apply=%region_8.9 | all-reduce | flops 1 | bytes 8 | tf_op jit(solution)/shard_map/psum | solution.py:38
  81.5 9.0 %psum.38 = f32[]{:T(128)} all-reduce(f32[]{:T(128)} %psum.37), channel_id=1, replica_groups=mesh['gx_0'=4,'gx_1'=4,'gy_0'=2,'gy_1'=4,'gy_2'=2] {'gy_1'}, use_global_device_ids=true, to_apply=%region_9.10 | all-reduce | flops 1 | bytes 8 | tf_op jit(solution)/shard_map/psum | solution.py:38
  90.6 10.3 %psum.39 = f32[]{:T(128)} all-reduce(f32[]{:T(128)} %psum.38), channel_id=1, replica_groups=mesh['gx_0'=4,'gx_1'=4,'gy_0'=2,'gy_1'=4,'gy_2'=2] {'gy_2'}, use_global_device_ids=true, to_apply=%region_10.11 | all-reduce | flops 1 | bytes 8 | tf_op jit(solution)/shard_map/psum | solution.py:38
  101.6 0.5 log_subtract_fusion
  102.1 0.8 convolution_divide_fusion
  (9 shorter events, 0.1 us)
Async XLA Ops:
  1.8 0.7 copy-start.1
  17.2 15.7 %copy-start = (bf16[128,128]{1,0:T(8,128)(2,1)S(1)}, bf16[128,128]{1,0:T(8,128)(2,1)}, u32[]{:S(2)}) copy-start(bf16[128,128]{1,0:T(8,128)(2,1)} %param.3) | copy-start | bytes 98308
  17.2 31.1 %all-to-all-start = ((f32[256,2,1,1,2]{4,1,3,2,0:T(2,128)}), f32[256,2,1,1,2]{4,1,3,2,0:T(2,128)S(1)}, u32[]{:S(2)}, u32[]{:S(2)}) async-start(f32[256,2,1,1,2]{4,1,3,2,0:T(2,128)} %copy.5), calls=%async_computation | async-start | bytes 524288 | tf_op jit(solution)/shard_map/all_to_all | solution.py:31
  48.3 53.8 %all-to-all-start.1 = ((bf16[256,1,1,2,128]{4,3,2,1,0:T(2,128)(2,1)}), bf16[256,1,1,2,128]{4,3,2,1,0:T(2,128)(2,1)S(1)}, u32[]{:S(2)}, u32[]{:S(2)}) async-start(bf16[256,1,1,2,128]{4,3,2,1,0:T(2,128)(2,1)} %bitcast.12), calls=%async_computation.1 | async-start | bytes 262144 | tf_op jit(solution)/shard_map/all_to_all | solution.py:31
where the time goes:
time: 103 us
  blocking collectives  45.5 us (44%)
  starting transfers between devices  21.5 us (21%)
  local copies, waits for them, and re-layouts  15.7 us (15%)
  waiting for transfers between devices  13.8 us (13%)
  other arithmetic  3.24 us (3%)
  matrix products  1.68 us (2%)
  between operations  1.45 us (1%)
    psum x5, blocking collectives, over_axes(): array = lax.psum(array, axis)  45.5 us
    all_to_all x2, starting transfers between devices, exchange_both(): tiles = lax.all_to_all(tiles, axis, split_axis=0, concat_axis=0, tiled=True)  21.5 us
    all_to_all x2, waiting for transfers between devices, exchange_both(): tiles = lax.all_to_all(tiles, axis, split_axis=0, concat_axis=0, tiled=True)  13.8 us
    scatter x2, local copies, waits for them, and re-layouts, shards(): tagging.at[0, slots].set(goal_weights).at[1, slots]  13.7 us
  transfers between devices with their start and end apart: 2, of which 1 were waited for; matrix products, arithmetic and copies ran while one was open for 3% of the time, Pallas kernels for 0%

commit v1 on v0

v1 whole, which is shorter than its diff:
```python
import jax
import jax.numpy as jnp
from jax import lax
from jax.experimental import pallas as pl
from jax.experimental.pallas import tpu as pltpu
from jax.sharding import Mesh
from jax.sharding import PartitionSpec as P

BINS_DEV = 64
GX_GY = ("gx_0", "gx_1", "gy_0", "gy_1", "gy_2")
LOGICAL = pl.DeviceIdType.LOGICAL
DEVICES = 256
PLANE = 32
DEPTH = 8


def depth_of(flat):
    return ((flat >> 6) << 1) | ((flat >> 3) & 1)


def place_of(flat):
    return (((flat >> 4) & 3) << 3) | (flat & 7)


def flat_of_place(place):
    return ((place >> 3) << 4) | (place & 7)


def flat_of_depth(depth):
    return ((depth >> 1) << 6) | ((depth & 1) << 3)


def remote(src, dst, send, recv, target):
    return pltpu.make_async_remote_copy(
        src_ref=src, dst_ref=dst, send_sem=send, recv_sem=recv, device_id=target, device_id_type=LOGICAL
    )


def exchange(
    embed_hbm, bins_hbm, weights_hbm, sums_ref, den_ref, log_ref,
    embed, bins, weights, packed, arrived, tags, plane_tags, column, depth_tags,
    in_sems, local_sems, send, recv, send_plane, recv_plane, send_depth, recv_depth,
):
    me = lax.axis_index(GX_GY)
    my_depth = depth_of(me)
    my_place = place_of(me)
    loads = [
        pltpu.make_async_copy(bins_hbm, bins, in_sems.at[0]),
        pltpu.make_async_copy(weights_hbm, weights, in_sems.at[1]),
        pltpu.make_async_copy(embed_hbm, embed, in_sems.at[2]),
    ]
    for load in loads:
        load.start()
    barrier = pltpu.get_barrier_semaphore()

    def greet(step, carry):
        pl.semaphore_signal(barrier, inc=1, device_id=me ^ (DEVICES - 1 - step), device_id_type=LOGICAL)
        return carry

    lax.fori_loop(0, DEVICES - 1, greet, 0, unroll=15)
    for load in loads:
        load.wait()

    lanes = lax.broadcasted_iota(jnp.int32, (128, 128), 1)
    rows = lax.broadcasted_iota(jnp.int32, (128, 128), 0)
    bin_row = jnp.broadcast_to(bins[...], (128, 128))
    weight_row = jnp.broadcast_to(weights[...], (128, 128))
    bin_col = jnp.transpose(bin_row.astype(jnp.float32)).astype(jnp.int32)
    weight_col = jnp.transpose(weight_row)
    owner_row = bin_row >> 6
    owner_col = bin_col >> 6
    earlier = jnp.where((owner_row == owner_col) & (rows < lanes), 1.0, 0.0)
    slot_of = jnp.sum(earlier, axis=0, keepdims=True).astype(jnp.int32)
    owner = bins[...] >> 6
    row_id = owner * 2 + slot_of
    tag_id = place_of(owner) * 2 + slot_of

    scaled = (weight_col * embed[...].astype(jnp.float32)).astype(jnp.bfloat16)
    pick = (lax.broadcasted_iota(jnp.int32, (2 * DEVICES, 128), 0) == row_id).astype(jnp.float32)
    packed[...] = jnp.dot(
        pick.astype(jnp.bfloat16), scaled, preferred_element_type=jnp.float32
    ).astype(jnp.bfloat16)

    lane_of = depth_of(owner_col) * 2
    offset_col = (bin_col & (BINS_DEV - 1)).astype(jnp.float32)
    values = jnp.where(lanes == lane_of, weight_col, 0.0) + jnp.where(lanes == lane_of + 1, offset_col, 0.0)
    tag_pick = (lax.broadcasted_iota(jnp.int32, (2 * PLANE, 128), 0) == tag_id).astype(jnp.float32)
    tag_lanes = lax.broadcasted_iota(jnp.int32, (2 * PLANE, 128), 1)
    tag_rows = lax.broadcasted_iota(jnp.int32, (2 * PLANE, 128), 0)
    local_total = jnp.sum(weights[...])
    tags[...] = jnp.dot(
        tag_pick, values, precision=lax.Precision.HIGHEST, preferred_element_type=jnp.float32
    ) + jnp.where((tag_lanes == 2 * DEPTH) & (tag_rows % 2 == 0), local_total, 0.0)

    pl.semaphore_wait(barrier, DEVICES - 1)

    for step in range(PLANE - 1, 0, -1):
        place = my_place ^ step
        remote(
            tags.at[pl.ds(pl.multiple_of(2 * place, 2), 2)],
            plane_tags.at[pl.ds(pl.multiple_of(2 * my_place, 2), 2)],
            send_plane, recv_plane, me ^ flat_of_place(step),
        ).start()
    my_slab = pl.ds(pl.multiple_of(2 * (my_depth * PLANE + my_place), 2), 2)

    def give(step, carry):
        target = me ^ (DEVICES - 1 - step)
        remote(
            packed.at[pl.ds(pl.multiple_of(2 * target, 2), 2)], arrived.at[my_slab], send, recv, target
        ).start()
        return carry

    lax.fori_loop(0, DEVICES - 1, give, 0, unroll=15)
    own = [
        pltpu.make_async_copy(packed.at[pl.ds(pl.multiple_of(2 * me, 2), 2)], arrived.at[my_slab], local_sems.at[0]),
        pltpu.make_async_copy(
            tags.at[pl.ds(pl.multiple_of(2 * my_place, 2), 2)],
            plane_tags.at[pl.ds(pl.multiple_of(2 * my_place, 2), 2)],
            local_sems.at[1],
        ),
    ]
    for copy in own:
        copy.start()
    for copy in own:
        copy.wait()

    others = pl.ds(0, 2 * (PLANE - 1))
    plane_all = remote(tags.at[others], plane_tags.at[others], send_plane, recv_plane, me ^ 1)
    plane_all.wait_recv()
    plane = plane_tags[...]
    plane_total = jnp.sum(jnp.where(tag_lanes == 2 * DEPTH, plane, 0.0))
    spare = jnp.where((tag_lanes < 2 * DEPTH) & (tag_lanes % 2 == 0) & (tag_rows == 0), plane_total, 0.0)
    column[...] = jnp.transpose(jnp.concatenate([plane, spare], axis=0))[: 2 * DEPTH]
    for step in range(DEPTH - 1, 0, -1):
        depth = my_depth ^ step
        remote(
            column.at[pl.ds(pl.multiple_of(2 * depth, 2), 2)],
            depth_tags.at[pl.ds(pl.multiple_of(2 * my_depth, 2), 2)],
            send_depth, recv_depth, me ^ flat_of_depth(step),
        ).start()
    mine = pl.ds(pl.multiple_of(2 * my_depth, 2), 2)
    own_column = pltpu.make_async_copy(column.at[mine], depth_tags.at[mine], local_sems.at[2])
    own_column.start()
    own_column.wait()
    others = pl.ds(0, 2 * (DEPTH - 1))
    depth_all = remote(column.at[others], depth_tags.at[others], send_depth, recv_depth, me ^ 8)
    depth_all.wait_recv()

    half = lax.broadcasted_iota(jnp.int32, (1, 128), 1) < 64
    labels = lax.broadcasted_iota(jnp.int32, (BINS_DEV, 128), 0).astype(jnp.float32)
    total = jnp.zeros((1, 1), jnp.float32)
    weighed = jnp.zeros((BINS_DEV, 128), jnp.float32)
    selectors = []
    for pair in range(DEPTH // 2):
        first = depth_tags[4 * pair : 4 * pair + 2]
        second = depth_tags[4 * pair + 2 : 4 * pair + 4]
        total = total + first[0:1, 64:65] + second[0:1, 64:65]
        turned = pltpu.roll(second, 64, axis=1)
        weight = jnp.where(half, first[0:1], turned[0:1])
        offset = jnp.where(half, first[1:2], turned[1:2])
        chosen = labels == offset
        weighed = weighed + jnp.where(chosen, weight, 0.0)
        selectors.append(jnp.where(chosen, 1.0, 0.0).astype(jnp.bfloat16))
    den = jnp.broadcast_to(jnp.sum(weighed, axis=1, keepdims=True), (BINS_DEV, 128)) + 1.0
    den_ref[...] = den
    logs = jnp.log(jnp.transpose(den)[0:1, :BINS_DEV])
    log_ref[...] = jnp.concatenate(
        [jnp.broadcast_to(jnp.log(total / (BINS_DEV * DEVICES)), (1, BINS_DEV)), logs], axis=1
    )

    most = pl.ds(0, 2 * (DEVICES - 1))
    all_data = remote(packed.at[most], arrived.at[most], send, recv, me ^ 1)
    all_data.wait_recv()
    sums_ref[...] = jnp.dot(
        jnp.concatenate(selectors, axis=1), arrived[...], preferred_element_type=jnp.float32
    )
    plane_all.wait_send()
    depth_all.wait_send()
    all_data.wait_send()


def shards(goal_embed, goal_bins, goal_weights):
    width = goal_embed.shape[1]
    goals = goal_embed.shape[0]
    vmem = pl.BlockSpec(memory_space=pltpu.VMEM)
    anywhere = pl.BlockSpec(memory_space=pl.ANY)
    dma = pltpu.SemaphoreType.DMA
    sums, den, logs = pl.pallas_call(
        exchange,
        out_shape=(
            jax.ShapeDtypeStruct((BINS_DEV, width), jnp.float32),
            jax.ShapeDtypeStruct((BINS_DEV, width), jnp.float32),
            jax.ShapeDtypeStruct((1, 2 * BINS_DEV), jnp.float32),
        ),
        in_specs=[anywhere] * 3,
        out_specs=(vmem, vmem, vmem),
        scratch_shapes=[
            pltpu.VMEM((goals, width), jnp.bfloat16),
            pltpu.VMEM((1, goals), jnp.int32),
            pltpu.VMEM((1, goals), jnp.float32),
            pltpu.VMEM((2 * DEVICES, width), jnp.bfloat16),
            pltpu.VMEM((2 * DEVICES, width), jnp.bfloat16),
            pltpu.VMEM((2 * PLANE, 128), jnp.float32),
            pltpu.VMEM((2 * PLANE, 128), jnp.float32),
            pltpu.VMEM((2 * DEPTH, 128), jnp.float32),
            pltpu.VMEM((2 * DEPTH, 128), jnp.float32),
            dma((3,)), dma((3,)),
            dma(()), dma(()), dma(()), dma(()), dma(()), dma(()),
        ],
        compiler_params=pltpu.CompilerParams(collective_id=0, has_side_effects=True),
        name="exchange",
    )(goal_embed, goal_bins.reshape(1, goals), goal_weights.reshape(1, goals))
    rarity = logs[0, :BINS_DEV] - logs[0, BINS_DEV:]
    return sums / den, rarity


def solution(mesh):
    split = Mesh(mesh.devices.reshape(4, 4, 2, 4, 2), GX_GY)
    placed = (P(GX_GY, None), P(GX_GY), P(GX_GY))
    return jax.shard_map(
        shards, mesh=split, in_specs=placed, out_specs=(P(GX_GY, None), P(GX_GY)), check_vma=False
    )
```

time: 103 us -> 25.1 us (0.24)
  blocking collectives: 45.5 us -> 0 us
  Pallas kernels: 0 us -> 22.3 us
  starting transfers between devices: 21.5 us -> 0 us
  local copies, waits for them, and re-layouts: 15.7 us -> 0.01 us
  waiting for transfers between devices: 13.8 us -> 0 us
  matrix products: 1.68 us -> 0 us
  other arithmetic: 3.24 us -> 1.98 us
    psum x5 -> x0, blocking collectives: 45.5 us -> none  [over_axes(): array = lax.psum(array, axis)]
    pallas_call x0 -> x1, Pallas kernels: none -> 22.3 us  [shards(): pl.pallas_call(exchange, out_shape=(jax.ShapeDtypeStruct((BINS_DEV, width...]
    all_to_all x2 -> x0, starting transfers between devices: 21.5 us -> none  [exchange_both(): tiles = lax.all_to_all(tiles, axis, split_axis=0, concat_axis=0, tiled=True)]
    all_to_all x2 -> x0, waiting for transfers between devices: 13.8 us -> none  [exchange_both(): tiles = lax.all_to_all(tiles, axis, split_axis=0, concat_axis=0, tiled=True)]
    scatter x2 -> x0, local copies, waits for them, and re-layouts: 13.7 us -> none  [shards(): tagging.at[0, slots].set(goal_weights).at[1, slots]]
    dot_general x2 -> x0, matrix products: 1.68 us -> none  [the longest x1 0.85 us: shards(): jnp.dot(selector.astype(jnp.float32), tag_rows[0], precision=lax.Precisio...]
    scatter x1 -> x0, other arithmetic: 1.59 us -> none  [shards(): jnp.zeros((devices * capacity, width), jnp.bfloat16).at[slots].set(scaled)]
    div x0 -> x1, other arithmetic: none -> 1.4 us  [shards(): return (sums / den, rarity)]
  transfers between devices with their start and end apart: 2 -> 0, of which waited for: 1 -> 0; matrix products, arithmetic and copies ran while one was open for 3% -> 0% of each run, Pallas kernels for 0% -> 0%
where the time goes in v1:
time: 25.1 us; the launch traced here: 25 us
  Pallas kernels  22.3 us (89%)
  other arithmetic  1.98 us (8%)
  between operations  0.65 us (3%)
    pallas_call x1, Pallas kernels, shards(): pl.pallas_call(exchange, out_shape=(jax.ShapeDtypeStruct((BINS_DEV, width...  22.3 us
    div x1, other arithmetic, shards(): return (sums / den, rarity)  1.4 us
    sub x1, other arithmetic, shards(): rarity = logs[0, :BINS_DEV] - logs[0, BINS_DEV:]  0.58 us

profile of v1, /device:TPU:1, one launch (start us, length us, event | category | flops | bytes accessed | tf_op | source)
XLA Modules:
  0.0 25.0 jit_solution(3946895000236654429)
XLA Ops:
  0.6 22.3 %exchange.1 = (f32[64,128]{1,0:T(8,128)}, f32[64,128]{1,0:T(8,128)}, f32[1,128]{1,0:T(1,128)}) custom-call(bf16[128,128]{1,0:T(8,128)(2,1)} %embed_hbm.1, s32[1,128]{1,0:T(1,128)} %bitcast.4, f32[1,128]{1,0:T(1,128)} %bitcast.5), custom_call_target="tpu_custom_call" | custom-call | tf_op jit(solution)/shard_map/exchange/pallas_call | solution.py:188
  23.0 0.0 copy-start
  23.0 1.4 %div.3 = f32[64,128]{1,0:T(8,128)} divide(f32[64,128]{1,0:T(8,128)} %get-tuple-element.5, f32[64,128]{1,0:T(8,128)} %get-tuple-element.6) | non-fusion elementwise | flops 8192 | bytes 98304 | tf_op jit(solution)/shard_map/div | solution.py:214
  24.4 0.0 copy-done
  24.4 0.6 %subtract_bitcast_fusion = f32[64]{0:T(128)} fusion(f32[1,128]{1,0:T(1,128)S(1)} %copy-done), kind=kLoop, calls=%fused_computation | loop fusion | flops 64 | bytes 768 | tf_op jit(solution)/shard_map/sub | solution.py:213
Async XLA Ops:
  23.0 1.4 %copy-start = (f32[1,128]{1,0:T(1,128)S(1)}, f32[1,128]{1,0:T(1,128)}, u32[]{:S(2)}) copy-start(f32[1,128]{1,0:T(1,128)} %get-tuple-element.7) | copy-start | bytes 1540

commit v2 on v1

v2 whole, which is shorter than its diff:
```python
import jax
import jax.numpy as jnp
from jax import lax
from jax.experimental import pallas as pl
from jax.experimental.pallas import tpu as pltpu
from jax.sharding import Mesh
from jax.sharding import PartitionSpec as P

BINS_DEV = 64
GX_GY = ("gx_0", "gx_1", "gy_0", "gy_1", "gy_2")
LOGICAL = pl.DeviceIdType.LOGICAL
DEVICES = 256
PLANE = 32
DEPTH = 8
HOPS = (0, 1, 2, 1)
STEPS = sorted(range(1, PLANE), key=lambda step: -(2 * HOPS[step >> 3] + 2 * HOPS[(step >> 1) & 3] + step % 2))
TURNS = (4, 3, 5, 2, 6, 1, 7)


def depth_of(flat):
    return ((flat >> 6) << 1) | ((flat >> 3) & 1)


def place_of(flat):
    return (((flat >> 4) & 3) << 3) | (flat & 7)


def flat_of_place(place):
    return ((place >> 3) << 4) | (place & 7)


def flat_of_depth(depth):
    return ((depth >> 1) << 6) | ((depth & 1) << 3)


def remote(src, dst, send, recv, target):
    return pltpu.make_async_remote_copy(
        src_ref=src, dst_ref=dst, send_sem=send, recv_sem=recv, device_id=target, device_id_type=LOGICAL
    )


def exchange(
    embed_hbm, bins_hbm, weights_hbm, sums_ref, den_ref, log_ref,
    embed, bins, weights, packed, relay, arrived, tags, plane_tags, column, depth_tags,
    in_sems, send_plane, recv_plane, send_depth, recv_depth, send_tags, recv_tags, send_column, recv_column,
):
    me = lax.axis_index(GX_GY)
    my_depth = depth_of(me)
    my_place = place_of(me)
    my_row = my_place >> 3
    bottom = flat_of_place(my_place)
    loads = [
        pltpu.make_async_copy(bins_hbm, bins, in_sems.at[0]),
        pltpu.make_async_copy(weights_hbm, weights, in_sems.at[1]),
        pltpu.make_async_copy(embed_hbm, embed, in_sems.at[2]),
    ]
    for load in loads:
        load.start()
    barrier = pltpu.get_barrier_semaphore()
    for turn in TURNS:
        depth = (my_depth + turn) & (DEPTH - 1)
        pl.semaphore_signal(barrier, inc=1, device_id=bottom | flat_of_depth(depth), device_id_type=LOGICAL)
    for step in STEPS:
        pl.semaphore_signal(barrier, inc=1, device_id=me ^ flat_of_place(step), device_id_type=LOGICAL)
    for load in loads:
        load.wait()

    lanes = lax.broadcasted_iota(jnp.int32, (128, 128), 1)
    rows = lax.broadcasted_iota(jnp.int32, (128, 128), 0)
    bin_row = jnp.broadcast_to(bins[...], (128, 128))
    weight_row = jnp.broadcast_to(weights[...], (128, 128))
    bin_col = jnp.transpose(bin_row.astype(jnp.float32)).astype(jnp.int32)
    weight_col = jnp.transpose(weight_row)
    owner_row = bin_row >> 6
    owner_col = bin_col >> 6
    earlier = jnp.where((owner_row == owner_col) & (rows < lanes), 1.0, 0.0)
    slot_of = jnp.sum(earlier, axis=0, keepdims=True).astype(jnp.int32)
    owner = bins[...] >> 6
    row_id = (place_of(owner) * DEPTH + depth_of(owner)) * 2 + slot_of
    tag_id = place_of(owner) * 2 + slot_of

    lane_of = depth_of(owner_col) * 2
    offset_col = (bin_col & (BINS_DEV - 1)).astype(jnp.float32)
    values = jnp.where(lanes == lane_of, weight_col, 0.0) + jnp.where(lanes == lane_of + 1, offset_col, 0.0)
    tag_pick = (lax.broadcasted_iota(jnp.int32, (2 * PLANE, 128), 0) == tag_id).astype(jnp.float32)
    tag_lanes = lax.broadcasted_iota(jnp.int32, (2 * PLANE, 128), 1)
    tag_rows = lax.broadcasted_iota(jnp.int32, (2 * PLANE, 128), 0)
    local_total = jnp.sum(weights[...])
    tags[...] = jnp.dot(
        tag_pick, values, precision=lax.Precision.HIGHEST, preferred_element_type=jnp.float32
    ) + jnp.where((tag_lanes == 2 * DEPTH) & (tag_rows % 2 == 0), local_total, 0.0)

    scaled = (weight_col * embed[...].astype(jnp.float32)).astype(jnp.bfloat16)
    pick = (lax.broadcasted_iota(jnp.int32, (2 * DEVICES, 128), 0) == row_id).astype(jnp.float32)
    packed.reshape(2 * DEVICES, 128)[...] = jnp.dot(
        pick.astype(jnp.bfloat16), scaled, preferred_element_type=jnp.float32
    ).astype(jnp.bfloat16)

    pl.semaphore_wait(barrier, PLANE - 1 + DEPTH - 1)

    my_tags = pl.ds(pl.multiple_of(2 * my_place, 2), 2)
    for step in STEPS:
        place = my_place ^ step
        remote(
            tags.at[pl.ds(pl.multiple_of(2 * place, 2), 2)], plane_tags.at[my_tags],
            send_tags, recv_tags, me ^ flat_of_place(step),
        ).start()
    for step in STEPS:
        remote(
            packed.at[my_place ^ step], relay.at[my_place],
            send_plane, recv_plane.at[step >> 3], me ^ flat_of_place(step),
        ).start()
    relay[my_place] = packed[my_place]
    plane_tags[my_tags] = tags[my_tags]

    def pass_on(group):
        count = 8 if group else 7
        remote(
            packed.at[pl.ds(0, count)], relay.at[pl.ds(0, count)], send_plane, recv_plane.at[group], me ^ 1
        ).wait_recv()
        members = pl.ds(pl.multiple_of((my_row ^ group) * 8, 8), 8)
        for turn in TURNS:
            depth = (my_depth + turn) & (DEPTH - 1)
            remote(
                relay.at[members, depth], arrived.at[my_depth, members],
                send_depth, recv_depth, bottom | flat_of_depth(depth),
            ).start()
        arrived[my_depth, members] = relay[members, my_depth]

    for group in (0, 1, 3):
        pass_on(group)

    others = pl.ds(0, 2 * (PLANE - 1))
    plane_all = remote(tags.at[others], plane_tags.at[others], send_tags, recv_tags, me ^ 1)
    plane_all.wait_recv()
    plane = plane_tags[...]
    plane_total = jnp.sum(jnp.where(tag_lanes == 2 * DEPTH, plane, 0.0))
    spare = jnp.where((tag_lanes < 2 * DEPTH) & (tag_lanes % 2 == 0) & (tag_rows == 0), plane_total, 0.0)
    column[...] = jnp.transpose(jnp.concatenate([plane, spare], axis=0))[: 2 * DEPTH]
    mine = pl.ds(pl.multiple_of(2 * my_depth, 2), 2)
    for turn in TURNS:
        depth = (my_depth + turn) & (DEPTH - 1)
        remote(
            column.at[pl.ds(pl.multiple_of(2 * depth, 2), 2)], depth_tags.at[mine],
            send_column, recv_column, bottom | flat_of_depth(depth),
        ).start()
    depth_tags[mine] = column[mine]
    pass_on(2)

    others = pl.ds(0, 2 * (DEPTH - 1))
    depth_all = remote(column.at[others], depth_tags.at[others], send_column, recv_column, me ^ 8)
    depth_all.wait_recv()

    half = lax.broadcasted_iota(jnp.int32, (1, 128), 1) < 64
    labels = lax.broadcasted_iota(jnp.int32, (BINS_DEV, 128), 0).astype(jnp.float32)
    total = jnp.zeros((1, 1), jnp.float32)
    weighed = jnp.zeros((BINS_DEV, 128), jnp.float32)
    selectors = []
    for pair in range(DEPTH // 2):
        first = depth_tags[4 * pair : 4 * pair + 2]
        second = depth_tags[4 * pair + 2 : 4 * pair + 4]
        total = total + first[0:1, 64:65] + second[0:1, 64:65]
        turned = pltpu.roll(second, 64, axis=1)
        weight = jnp.where(half, first[0:1], turned[0:1])
        offset = jnp.where(half, first[1:2], turned[1:2])
        chosen = labels == offset
        weighed = weighed + jnp.where(chosen, weight, 0.0)
        selectors.append(jnp.where(chosen, 1.0, 0.0).astype(jnp.bfloat16))
    den = jnp.broadcast_to(jnp.sum(weighed, axis=1, keepdims=True), (BINS_DEV, 128)) + 1.0
    den_ref[...] = den
    logs = jnp.log(jnp.transpose(den)[0:1, :BINS_DEV])
    log_ref[...] = jnp.concatenate(
        [jnp.broadcast_to(jnp.log(total / (BINS_DEV * DEVICES)), (1, BINS_DEV)), logs], axis=1
    )

    depth_most = arrived.at[pl.ds(0, DEPTH - 1)]
    depth_data = remote(depth_most, depth_most, send_depth, recv_depth, me ^ 8)
    depth_data.wait_recv()
    sums_ref[...] = jnp.dot(
        jnp.concatenate(selectors, axis=1), arrived.reshape(2 * DEVICES, 128)[...],
        preferred_element_type=jnp.float32,
    )
    most = pl.ds(0, PLANE - 1)
    remote(packed.at[most], relay.at[most], send_plane, recv_plane.at[0], me ^ 1).wait_send()
    plane_all.wait_send()
    depth_all.wait_send()
    depth_data.wait_send()


def shards(goal_embed, goal_bins, goal_weights):
    width = goal_embed.shape[1]
    goals = goal_embed.shape[0]
    vmem = pl.BlockSpec(memory_space=pltpu.VMEM)
    anywhere = pl.BlockSpec(memory_space=pltpu.HBM)
    dma = pltpu.SemaphoreType.DMA
    sums, den, logs = pl.pallas_call(
        exchange,
        out_shape=(
            jax.ShapeDtypeStruct((BINS_DEV, width), jnp.float32),
            jax.ShapeDtypeStruct((BINS_DEV, width), jnp.float32),
            jax.ShapeDtypeStruct((1, 2 * BINS_DEV), jnp.float32),
        ),
        in_specs=[anywhere] * 3,
        out_specs=(vmem, vmem, vmem),
        scratch_shapes=[
            pltpu.VMEM((goals, width), jnp.bfloat16),
            pltpu.VMEM((1, goals), jnp.int32),
            pltpu.VMEM((1, goals), jnp.float32),
            pltpu.VMEM((PLANE, DEPTH, 2, width), jnp.bfloat16),
            pltpu.VMEM((PLANE, DEPTH, 2, width), jnp.bfloat16),
            pltpu.VMEM((DEPTH, PLANE, 2, width), jnp.bfloat16),
            pltpu.VMEM((2 * PLANE, 128), jnp.float32),
            pltpu.VMEM((2 * PLANE, 128), jnp.float32),
            pltpu.VMEM((2 * DEPTH, 128), jnp.float32),
            pltpu.VMEM((2 * DEPTH, 128), jnp.float32),
            dma((3,)), dma(()), dma((4,)), dma(()), dma(()), dma(()), dma(()), dma(()), dma(()),
        ],
        compiler_params=pltpu.CompilerParams(collective_id=0, has_side_effects=True, vmem_limit_bytes=4 << 20),
        name="exchange",
    )(*[
        pltpu.with_memory_space_constraint(array, pltpu.HBM)
        for array in (goal_embed, goal_bins.reshape(1, goals), goal_weights.reshape(1, goals))
    ])
    rarity = logs[0, :BINS_DEV] - logs[0, BINS_DEV:]
    return sums / den, rarity


def solution(mesh):
    split = Mesh(mesh.devices.reshape(4, 4, 2, 4, 2), GX_GY)
    placed = (P(GX_GY, None), P(GX_GY), P(GX_GY))
    return jax.shard_map(
        shards, mesh=split, in_specs=placed, out_specs=(P(GX_GY, None), P(GX_GY)), check_vma=False
    )
```

time: 25.1 us -> 22.8 us (0.908)
  Pallas kernels: 22.3 us -> 20.9 us
  other arithmetic: 1.98 us -> 1.21 us
    pallas_call x1, Pallas kernels: 22.3 us -> 20.9 us  [shards(): pl.pallas_call(exchange, out_shape=(jax.ShapeDtypeStruct((BINS_DEV, width...]
    div x1, other arithmetic: 1.4 us -> 0.63 us  [shards(): return (sums / den, rarity)]
where the time goes in v2:
time: 22.8 us; the launch traced here: 22.7 us
  Pallas kernels  20.9 us (92%)
  other arithmetic  1.21 us (5%)
  between operations  0.64 us (3%)
    pallas_call x1, Pallas kernels, shards(): pl.pallas_call(exchange, out_shape=(jax.ShapeDtypeStruct((BINS_DEV, width...  20.9 us
    div x1, other arithmetic, shards(): return (sums / den, rarity)  0.63 us
    sub x1, other arithmetic, shards(): rarity = logs[0, :BINS_DEV] - logs[0, BINS_DEV:]  0.58 us

profile of v2, /device:TPU:1, one launch (start us, length us, event | category | flops | bytes accessed | tf_op | source)
XLA Modules:
  0.0 22.7 jit_solution(8114119321151030197)
XLA Ops:
  0.6 20.9 %exchange.1 = (f32[64,128]{1,0:T(8,128)S(1)}, f32[64,128]{1,0:T(8,128)S(1)}, f32[1,128]{1,0:T(1,128)S(1)}) custom-call(bf16[128,128]{1,0:T(8,128)(2,1)} %embed_hbm.1, s32[1,128]{1,0:T(1,128)} %bitcast.4, f32[1,128]{1,0:T(1,128)} %bitcast.5), custom_call_target="tpu_custom_call" | custom-call | tf_op jit(solution)/shard_map/exchange/pallas_call | solution.py:196
  21.5 0.6 %div.3 = f32[64,128]{1,0:T(8,128)} divide(f32[64,128]{1,0:T(8,128)S(1)} %get-tuple-element.5, f32[64,128]{1,0:T(8,128)S(1)} %get-tuple-element.6) | non-fusion elementwise | flops 8192 | bytes 98304 | tf_op jit(solution)/shard_map/div | solution.py:225
  22.1 0.6 %subtract_bitcast_fusion = f32[64]{0:T(128)} fusion(f32[1,128]{1,0:T(1,128)S(1)} %get-tuple-element.7), kind=kLoop, calls=%fused_computation | loop fusion | flops 64 | bytes 768 | tf_op jit(solution)/shard_map/sub | solution.py:224

commit v3 on v2

v3 whole, which is shorter than its diff:
```python
import jax
import jax.numpy as jnp
from jax import lax
from jax.experimental import pallas as pl
from jax.experimental.pallas import tpu as pltpu
from jax.sharding import Mesh
from jax.sharding import PartitionSpec as P

BINS_DEV = 64
AXIS = "device"
LOGICAL = pl.DeviceIdType.LOGICAL
DEVICES = 256
CHIPS = 16
PLANE = 32
DEPTH = 8
HOPS = (0, 1, 2, 1)
STEPS = sorted(range(1, CHIPS), key=lambda step: -(HOPS[step >> 2] + HOPS[step & 3]))
GROUPS = (0, 3, 1, 2)


def depth_of(flat):
    return ((flat >> 6) << 1) | ((flat >> 3) & 1)


def chip_of(flat):
    return (((flat >> 4) & 3) << 2) | ((flat >> 1) & 3)


def flat_of_chip(chip):
    return ((chip >> 2) << 4) | ((chip & 3) << 1)


def flat_of_depth(depth):
    return ((depth >> 1) << 6) | ((depth & 1) << 3)


def remote(src, dst, send, recv, target):
    return pltpu.make_async_remote_copy(
        src_ref=src, dst_ref=dst, send_sem=send, recv_sem=recv, device_id=target, device_id_type=LOGICAL
    )


def two(index):
    return pl.ds(pl.multiple_of(2 * index, 2), 2)


def exchange(
    embed_hbm, bins_hbm, weights_hbm, mean_ref, rarity_ref,
    embed, bins, weights, packed, relay, arrived, tags, plane_tags, column, depth_tags,
    in_sems, send_plane, recv_plane, send_depth, recv_depth,
    send_tags, recv_tags, send_column, recv_column, column_ready,
):
    me = lax.axis_index(AXIS)
    core = me & 1
    my_depth = depth_of(me)
    my_chip = chip_of(me)
    my_place = my_chip * 2 + core
    my_row = my_chip >> 2
    bottom = flat_of_chip(my_chip)
    loads = [
        pltpu.make_async_copy(bins_hbm, bins, in_sems.at[0]),
        pltpu.make_async_copy(weights_hbm, weights, in_sems.at[1]),
        pltpu.make_async_copy(embed_hbm, embed, in_sems.at[2]),
    ]
    for load in loads:
        load.start()
    barrier = pltpu.get_barrier_semaphore()

    def greet(target):
        pl.semaphore_signal(barrier, inc=1, device_id=target, device_id_type=LOGICAL)

    def column_core(turn):
        depth = turn + (turn >= my_depth).astype(jnp.int32)
        return depth, bottom | flat_of_depth(depth) | 1

    greet(me ^ 1)

    @pl.when(core == 1)
    def _():
        for step in STEPS:
            greet(me ^ flat_of_chip(step))
            greet(me ^ flat_of_chip(step) ^ 1)
        for turn in range(DEPTH - 1):
            greet(column_core(turn)[1])

    for load in loads:
        load.wait()

    lanes = lax.broadcasted_iota(jnp.int32, (128, 128), 1)
    rows = lax.broadcasted_iota(jnp.int32, (128, 128), 0)
    bin_row = jnp.broadcast_to(bins[...], (128, 128))
    weight_row = jnp.broadcast_to(weights[...], (128, 128))
    bin_col = jnp.transpose(bin_row.astype(jnp.float32)).astype(jnp.int32)
    weight_col = jnp.transpose(weight_row)
    owner_row = bin_row >> 6
    owner_col = bin_col >> 6
    earlier = jnp.where((owner_row == owner_col) & (rows < lanes), 1.0, 0.0)
    slot_of = jnp.sum(earlier, axis=0, keepdims=True).astype(jnp.int32)
    owner = bins[...] >> 6
    row_id = ((chip_of(owner) * DEPTH + depth_of(owner)) * 2 + (owner & 1)) * 2 + slot_of
    tag_id = chip_of(owner) * 2 + slot_of

    lane_of = (depth_of(owner_col) * 2 + (owner_col & 1)) * 2
    offset_col = (bin_col & (BINS_DEV - 1)).astype(jnp.float32)
    values = jnp.where(lanes == lane_of, weight_col, 0.0) + jnp.where(lanes == lane_of + 1, offset_col, 0.0)
    tag_lanes = lax.broadcasted_iota(jnp.int32, (2 * CHIPS, 128), 1)
    tag_rows = lax.broadcasted_iota(jnp.int32, (2 * CHIPS, 128), 0)
    tag_pick = (tag_rows == tag_id).astype(jnp.float32)
    local_total = jnp.sum(weights[...])
    tags[...] = jnp.dot(
        tag_pick, values, precision=lax.Precision.HIGHEST, preferred_element_type=jnp.float32
    ) + jnp.where((tag_lanes == 4 * DEPTH) & (tag_rows % 2 == 0), local_total, 0.0)

    scaled = (weight_col * embed[...].astype(jnp.float32)).astype(jnp.bfloat16)
    pick = (lax.broadcasted_iota(jnp.int32, (2 * DEVICES, 128), 0) == row_id).astype(jnp.float32)
    packed.reshape(2 * DEVICES, 128)[...] = jnp.dot(
        pick.astype(jnp.bfloat16), scaled, preferred_element_type=jnp.float32
    ).astype(jnp.bfloat16)

    def hand_tags(chip, target):
        remote(tags.at[two(chip)], plane_tags.at[two(my_place)], send_tags, recv_tags, target).start()

    def hand_data(chip, target, group):
        remote(packed.at[chip], relay.at[my_place], send_plane, recv_plane.at[group], target).start()

    def hand_all():
        for step in STEPS:
            hand_tags(my_chip ^ step, (me ^ flat_of_chip(step)) | 1)
        for step in STEPS:
            hand_data(my_chip ^ step, (me ^ flat_of_chip(step)) | 1, step >> 2)

    everything = arrived.at[pl.ds(0, DEPTH)]
    all_tags = pl.ds(0, 2 * DEPTH)

    @pl.when(core == 0)
    def _():
        pl.semaphore_wait(barrier, CHIPS)
        hand_all()
        hand_tags(my_chip, me ^ 1)
        hand_data(my_chip, me ^ 1, 0)
        remote(depth_tags.at[all_tags], depth_tags.at[all_tags], send_column, recv_column, me ^ 1).wait_recv()

    @pl.when(core == 1)
    def _():
        pl.semaphore_wait(barrier, CHIPS - 1 + DEPTH - 1 + 1)
        hand_all()
        for turn in range(DEPTH - 1):
            pl.semaphore_signal(column_ready, inc=1, device_id=column_core(turn)[1], device_id_type=LOGICAL)
        relay[my_place] = packed[my_chip]
        plane_tags[two(my_place)] = tags[two(my_chip)]
        pl.semaphore_wait(column_ready, DEPTH - 1)

        def pass_on(group):
            count = 8 if group else 7
            part = relay.at[pl.ds(0, count)]
            remote(part, part, send_plane, recv_plane.at[group], me ^ 1).wait_recv()
            members = pl.ds(pl.multiple_of((my_row ^ group) * 8, 8), 8)
            for turn in range(DEPTH - 1):
                depth, target = column_core(turn)
                for side in (0, 1):
                    remote(
                        relay.at[members, depth * 2 + side], arrived.at[my_depth, members],
                        send_depth, recv_depth, target ^ 1 ^ side,
                    ).start()
            remote(
                relay.at[members, my_depth * 2], arrived.at[my_depth, members], send_depth, recv_depth, me ^ 1
            ).start()
            arrived[my_depth, members] = relay[members, my_depth * 2 + 1]

        for group in GROUPS[:3]:
            pass_on(group)

        others = plane_tags.at[pl.ds(0, 2 * (PLANE - 1))]
        remote(others, others, send_tags, recv_tags, me ^ 1).wait_recv()
        plane = plane_tags[...]
        wide_lanes = lax.broadcasted_iota(jnp.int32, (2 * PLANE, 128), 1)
        wide_rows = lax.broadcasted_iota(jnp.int32, (2 * PLANE, 128), 0)
        plane_total = jnp.sum(jnp.where(wide_lanes == 4 * DEPTH, plane, 0.0))
        spare = jnp.where(
            (wide_lanes < 4 * DEPTH) & (wide_lanes % 2 == 0) & (wide_rows == 0), plane_total, 0.0
        )
        column[...] = jnp.transpose(jnp.concatenate([plane, spare], axis=0))[: 4 * DEPTH]
        for turn in range(DEPTH - 1):
            depth, target = column_core(turn)
            for side in (0, 1):
                remote(
                    column.at[two(depth * 2 + side)], depth_tags.at[two(my_depth)],
                    send_column, recv_column, target ^ 1 ^ side,
                ).start()
        remote(
            column.at[two(my_depth * 2)], depth_tags.at[two(my_depth)], send_column, recv_column, me ^ 1
        ).start()
        depth_tags[two(my_depth)] = column[two(my_depth * 2 + 1)]
        pass_on(GROUPS[3])
        most = depth_tags.at[pl.ds(0, 2 * (DEPTH - 1))]
        remote(most, most, send_column, recv_column, me ^ 1).wait_recv()

    half = lax.broadcasted_iota(jnp.int32, (1, 128), 1) < 64
    labels = lax.broadcasted_iota(jnp.int32, (BINS_DEV, 128), 0).astype(jnp.float32)
    total = jnp.zeros((1, 1), jnp.float32)
    weighed = jnp.zeros((BINS_DEV, 128), jnp.float32)
    selectors = []
    for pair in range(DEPTH // 2):
        first = depth_tags[4 * pair : 4 * pair + 2]
        second = depth_tags[4 * pair + 2 : 4 * pair + 4]
        total = total + first[0:1, 64:65] + second[0:1, 64:65]
        turned = pltpu.roll(second, 64, axis=1)
        weight = jnp.where(half, first[0:1], turned[0:1])
        offset = jnp.where(half, first[1:2], turned[1:2])
        chosen = labels == offset
        weighed = weighed + jnp.where(chosen, weight, 0.0)
        selectors.append(jnp.where(chosen, 1.0, 0.0).astype(jnp.bfloat16))
    den = jnp.broadcast_to(jnp.sum(weighed, axis=1, keepdims=True), (BINS_DEV, 128)) + 1.0
    rarity_ref[...] = jnp.log(total / (BINS_DEV * DEVICES)) - jnp.log(jnp.transpose(den)[0:1, :BINS_DEV])

    @pl.when(core == 0)
    def _():
        remote(everything, everything, send_depth, recv_depth, me ^ 1).wait_recv()

    @pl.when(core == 1)
    def _():
        most = arrived.at[pl.ds(0, DEPTH - 1)]
        remote(most, most, send_depth, recv_depth, me ^ 1).wait_recv()

    mean_ref[...] = jnp.dot(
        jnp.concatenate(selectors, axis=1), arrived.reshape(2 * DEVICES, 128)[...],
        preferred_element_type=jnp.float32,
    ) / den

    def sent(chips):
        part = packed.at[pl.ds(0, chips)]
        remote(part, part, send_plane, recv_plane.at[0], me ^ 1).wait_send()
        part = tags.at[pl.ds(0, 2 * chips)]
        remote(part, part, send_tags, recv_tags, me ^ 1).wait_send()

    @pl.when(core == 0)
    def _():
        sent(CHIPS)

    @pl.when(core == 1)
    def _():
        sent(CHIPS - 1)
        part = relay.at[pl.ds(0, 2 * (2 * DEPTH - 1))]
        remote(part, part, send_depth, recv_depth, me ^ 1).wait_send()
        part = column.at[pl.ds(0, 2 * (2 * DEPTH - 1))]
        remote(part, part, send_column, recv_column, me ^ 1).wait_send()


def write_out(mean, rarity, mean_hbm, rarity_hbm, sems):
    copies = [
        pltpu.make_async_copy(mean, mean_hbm, sems.at[0]),
        pltpu.make_async_copy(rarity, rarity_hbm, sems.at[1]),
    ]
    for copy in copies:
        copy.start()
    for copy in copies:
        copy.wait()


def shards(goal_embed, goal_bins, goal_weights):
    width = goal_embed.shape[1]
    goals = goal_embed.shape[0]
    vmem = pl.BlockSpec(memory_space=pltpu.VMEM)
    hbm = pl.BlockSpec(memory_space=pltpu.HBM)
    dma = pltpu.SemaphoreType.DMA
    shapes = (
        jax.ShapeDtypeStruct((BINS_DEV, width), jnp.float32),
        jax.ShapeDtypeStruct((1, BINS_DEV), jnp.float32),
    )
    results = pl.pallas_call(
        exchange,
        out_shape=shapes,
        in_specs=[hbm] * 3,
        out_specs=(vmem, vmem),
        scratch_shapes=[
            pltpu.VMEM((goals, width), jnp.bfloat16),
            pltpu.VMEM((1, goals), jnp.int32),
            pltpu.VMEM((1, goals), jnp.float32),
            pltpu.VMEM((CHIPS, 2 * DEPTH, 2, width), jnp.bfloat16),
            pltpu.VMEM((PLANE, 2 * DEPTH, 2, width), jnp.bfloat16),
            pltpu.VMEM((DEPTH, PLANE, 2, width), jnp.bfloat16),
            pltpu.VMEM((2 * CHIPS, 128), jnp.float32),
            pltpu.VMEM((2 * PLANE, 128), jnp.float32),
            pltpu.VMEM((4 * DEPTH, 128), jnp.float32),
            pltpu.VMEM((2 * DEPTH, 128), jnp.float32),
            dma((3,)), dma(()), dma((4,)), dma(()), dma(()), dma(()), dma(()), dma(()), dma(()),
            pltpu.SemaphoreType.REGULAR,
        ],
        compiler_params=pltpu.CompilerParams(collective_id=0, has_side_effects=True, vmem_limit_bytes=4 << 20),
        name="exchange",
    )(*[
        pltpu.with_memory_space_constraint(array, pltpu.HBM)
        for array in (goal_embed, goal_bins.reshape(1, goals), goal_weights.reshape(1, goals))
    ])
    mean, rarity = pl.pallas_call(
        write_out,
        out_shape=shapes,
        in_specs=[vmem, vmem],
        out_specs=(hbm, hbm),
        scratch_shapes=[dma((2,))],
        compiler_params=pltpu.CompilerParams(vmem_limit_bytes=1 << 20),
        name="write_out",
    )(*results)
    return mean, rarity[0]


def solution(mesh):
    flat = Mesh(mesh.devices.reshape(-1), (AXIS,))
    return jax.shard_map(
        shards, mesh=flat, in_specs=(P(AXIS, None), P(AXIS), P(AXIS)),
        out_specs=(P(AXIS, None), P(AXIS)), check_vma=False,
    )
```

time: 22.8 us -> 21.4 us (0.939)
  other arithmetic: 1.21 us -> 0 us
  Pallas kernels: 20.9 us -> 20.6 us
    div x1 -> x0, other arithmetic: 0.63 us -> none  [shards(): return (sums / den, rarity)]
    sub x1 -> x0, other arithmetic: 0.58 us -> none  [shards(): rarity = logs[0, :BINS_DEV] - logs[0, BINS_DEV:]]
    pallas_call x1 -> x2, Pallas kernels: 20.9 us -> 20.6 us  [the longest x1 20 us: shards(): pl.pallas_call(exchange, out_shape=shapes, in_specs=[hbm] * 3, out_specs=...]
where the time goes in v3:
time: 21.4 us; the launch traced here: 21.3 us
  Pallas kernels  20.6 us (96%)
  between operations  0.64 us (3%)
    pallas_call x1, Pallas kernels, shards(): pl.pallas_call(exchange, out_shape=shapes, in_specs=[hbm] * 3, out_specs=...  20 us
    pallas_call x1, Pallas kernels, shards(): pl.pallas_call(write_out, out_shape=shapes, in_specs=[vmem, vmem], out_sp...  0.64 us

profile of v3, /device:TPU:1, one launch (start us, length us, event | category | flops | bytes accessed | tf_op | source)
XLA Modules:
  0.0 21.3 jit_solution(14024238630718375990)
XLA Ops:
  0.6 20.0 %exchange.1 = (f32[64,128]{1,0:T(8,128)S(1)}, f32[1,64]{1,0:T(1,128)S(1)}) custom-call(bf16[128,128]{1,0:T(8,128)(2,1)} %embed_hbm.1, s32[1,128]{1,0:T(1,128)} %bitcast.3, f32[1,128]{1,0:T(1,128)} %bitcast.4), custom_call_target="tpu_custom_call" | custom-call | tf_op jit(solution)/shard_map/exchange/pallas_call | solution.py:270
  20.6 0.6 %write_out.1 = (f32[64,128]{1,0:T(8,128)}, f32[1,64]{1,0:T(1,128)}) custom-call(f32[64,128]{1,0:T(8,128)S(1)} %get-tuple-element.6.mean, f32[1,64]{1,0:T(1,128)S(1)} %get-tuple-element.7.rarity), custom_call_target="tpu_custom_call" | custom-call | tf_op jit(solution)/shard_map/write_out/pallas_call | solution.py:295

commit v4 on v3

--- a/solution.py
+++ b/solution.py
@@ -1,3 +1,5 @@
+import functools
+
 import jax
 import jax.numpy as jnp
 from jax import lax
@@ -16,6 +18,9 @@
 HOPS = (0, 1, 2, 1)
 STEPS = sorted(range(1, CHIPS), key=lambda step: -(HOPS[step >> 2] + HOPS[step & 3]))
 GROUPS = (0, 3, 1, 2)
+FIRST = 1
+FIRST_LOTS = pl.ds(0, 2 * FIRST)
+REST_LOTS = pl.ds(2 * FIRST, 2 * (DEPTH - FIRST))
 
 
 def depth_of(flat):
@@ -47,7 +52,7 @@
 def exchange(
     embed_hbm, bins_hbm, weights_hbm, mean_ref, rarity_ref,
     embed, bins, weights, packed, relay, arrived, tags, plane_tags, column, depth_tags,
-    in_sems, send_plane, recv_plane, send_depth, recv_depth,
+    in_sems, send_plane, recv_plane, recv_rest, send_depth, recv_depth,
     send_tags, recv_tags, send_column, recv_column, column_ready,
 ):
     me = lax.axis_index(AXIS)
@@ -69,9 +74,8 @@
     def greet(target):
         pl.semaphore_signal(barrier, inc=1, device_id=target, device_id_type=LOGICAL)
 
-    def column_core(turn):
-        depth = turn + (turn >= my_depth).astype(jnp.int32)
-        return depth, bottom | flat_of_depth(depth) | 1
+    def other_relay(turn):
+        return bottom | flat_of_depth(turn + (turn >= my_depth).astype(jnp.int32)) | 1
 
     greet(me ^ 1)
 
@@ -81,7 +85,7 @@
             greet(me ^ flat_of_chip(step))
             greet(me ^ flat_of_chip(step) ^ 1)
         for turn in range(DEPTH - 1):
-            greet(column_core(turn)[1])
+            greet(other_relay(turn))
 
     for load in loads:
         load.wait()
@@ -120,14 +124,21 @@
     def hand_tags(chip, target):
         remote(tags.at[two(chip)], plane_tags.at[two(my_place)], send_tags, recv_tags, target).start()
 
-    def hand_data(chip, target, group):
-        remote(packed.at[chip], relay.at[my_place], send_plane, recv_plane.at[group], target).start()
+    def hand_first(chip, target, group):
+        remote(
+            packed.at[chip, FIRST_LOTS], relay.at[my_place, FIRST_LOTS],
+            send_plane, recv_plane.at[group], target,
+        ).start()
+
+    def hand_rest(chip, target):
+        remote(
+            packed.at[chip, REST_LOTS], relay.at[my_place, REST_LOTS], send_plane, recv_rest, target
+        ).start()
 
     def hand_all():
         for step in STEPS:
             hand_tags(my_chip ^ step, (me ^ flat_of_chip(step)) | 1)
-        for step in STEPS:
-            hand_data(my_chip ^ step, (me ^ flat_of_chip(step)) | 1, step >> 2)
+            hand_first(my_chip ^ step, (me ^ flat_of_chip(step)) | 1, step >> 2)
 
     everything = arrived.at[pl.ds(0, DEPTH)]
     all_tags = pl.ds(0, 2 * DEPTH)
@@ -137,35 +148,42 @@
         pl.semaphore_wait(barrier, CHIPS)
         hand_all()
         hand_tags(my_chip, me ^ 1)
-        hand_data(my_chip, me ^ 1, 0)
+        hand_first(my_chip, me ^ 1, 0)
+        for step in STEPS:
+            hand_rest(my_chip ^ step, (me ^ flat_of_chip(step)) | 1)
+        hand_rest(my_chip, me ^ 1)
         remote(depth_tags.at[all_tags], depth_tags.at[all_tags], send_column, recv_column, me ^ 1).wait_recv()
 
     @pl.when(core == 1)
     def _():
         pl.semaphore_wait(barrier, CHIPS - 1 + DEPTH - 1 + 1)
         hand_all()
+        for step in STEPS:
+            hand_rest(my_chip ^ step, (me ^ flat_of_chip(step)) | 1)
         for turn in range(DEPTH - 1):
-            pl.semaphore_signal(column_ready, inc=1, device_id=column_core(turn)[1], device_id_type=LOGICAL)
+            pl.semaphore_signal(column_ready, inc=1, device_id=other_relay(turn), device_id_type=LOGICAL)
         relay[my_place] = packed[my_chip]
         plane_tags[two(my_place)] = tags[two(my_chip)]
         pl.semaphore_wait(column_ready, DEPTH - 1)
 
+        def both_cores(depths, send_to):
+            for depth in depths:
+                column_at = bottom | flat_of_depth(depth)
+                send_to(column_at, 2 * depth)
+                pl.when(my_depth != depth)(functools.partial(send_to, column_at | 1, 2 * depth + 1))
+
         def pass_on(group):
             count = 8 if group else 7
-            part = relay.at[pl.ds(0, count)]
+            part = relay.at[pl.ds(0, count), FIRST_LOTS]
             remote(part, part, send_plane, recv_plane.at[group], me ^ 1).wait_recv()
             members = pl.ds(pl.multiple_of((my_row ^ group) * 8, 8), 8)
-            for turn in range(DEPTH - 1):
-                depth, target = column_core(turn)
-                for side in (0, 1):
-                    remote(
-                        relay.at[members, depth * 2 + side], arrived.at[my_depth, members],
-                        send_depth, recv_depth, target ^ 1 ^ side,
-                    ).start()
-            remote(
-                relay.at[members, my_depth * 2], arrived.at[my_depth, members], send_depth, recv_depth, me ^ 1
-            ).start()
-            arrived[my_depth, members] = relay[members, my_depth * 2 + 1]
+
+            def send_to(target, lot):
+                remote(
+                    relay.at[members, lot], arrived.at[my_depth, members], send_depth, recv_depth, target
+                ).start()
+
+            both_cores(range(FIRST), send_to)
 
         for group in GROUPS[:3]:
             pass_on(group)
@@ -180,18 +198,23 @@
             (wide_lanes < 4 * DEPTH) & (wide_lanes % 2 == 0) & (wide_rows == 0), plane_total, 0.0
         )
         column[...] = jnp.transpose(jnp.concatenate([plane, spare], axis=0))[: 4 * DEPTH]
-        for turn in range(DEPTH - 1):
-            depth, target = column_core(turn)
-            for side in (0, 1):
-                remote(
-                    column.at[two(depth * 2 + side)], depth_tags.at[two(my_depth)],
-                    send_column, recv_column, target ^ 1 ^ side,
-                ).start()
-        remote(
-            column.at[two(my_depth * 2)], depth_tags.at[two(my_depth)], send_column, recv_column, me ^ 1
-        ).start()
+
+        def send_column_to(target, lot):
+            remote(
+                column.at[two(lot)], depth_tags.at[two(my_depth)], send_column, recv_column, target
+            ).start()
+
+        both_cores(range(DEPTH), send_column_to)
         depth_tags[two(my_depth)] = column[two(my_depth * 2 + 1)]
         pass_on(GROUPS[3])
+        part = relay.at[pl.ds(0, PLANE - 1), REST_LOTS]
+        remote(part, part, send_plane, recv_rest, me ^ 1).wait_recv()
+
+        def send_rest_to(target, lot):
+            remote(relay.at[:, lot], arrived.at[my_depth], send_depth, recv_depth, target).start()
+
+        both_cores(range(FIRST, DEPTH), send_rest_to)
+        arrived[my_depth] = relay[:, my_depth * 2 + 1]
         most = depth_tags.at[pl.ds(0, 2 * (DEPTH - 1))]
         remote(most, most, send_column, recv_column, me ^ 1).wait_recv()
 
@@ -283,7 +306,7 @@
             pltpu.VMEM((2 * PLANE, 128), jnp.float32),
             pltpu.VMEM((4 * DEPTH, 128), jnp.float32),
             pltpu.VMEM((2 * DEPTH, 128), jnp.float32),
-            dma((3,)), dma(()), dma((4,)), dma(()), dma(()), dma(()), dma(()), dma(()), dma(()),
+            dma((3,)), dma(()), dma((4,)), dma(()), dma(()), dma(()), dma(()), dma(()), dma(()), dma(()),
             pltpu.SemaphoreType.REGULAR,
         ],
         compiler_params=pltpu.CompilerParams(collective_id=0, has_side_effects=True, vmem_limit_bytes=4 << 20),

time: 21.4 us -> 20.1 us (0.939)
  Pallas kernels: 20.6 us -> 19.3 us
    pallas_call x1, Pallas kernels: 20 us -> 18.7 us  [shards(): pl.pallas_call(exchange, out_shape=shapes, in_specs=[hbm] * 3, out_specs=...]
where the time goes in v4:
time: 20.1 us; the launch traced here: 20 us
  Pallas kernels  19.3 us (96%)
  between operations  0.64 us (3%)
    pallas_call x1, Pallas kernels, shards(): pl.pallas_call(exchange, out_shape=shapes, in_specs=[hbm] * 3, out_specs=...  18.7 us
    pallas_call x1, Pallas kernels, shards(): pl.pallas_call(write_out, out_shape=shapes, in_specs=[vmem, vmem], out_sp...  0.64 us

profile of v4, /device:TPU:1, one launch (start us, length us, event | category | flops | bytes accessed | tf_op | source)
XLA Modules:
  0.0 20.0 jit_solution(11089065839721068304)
XLA Ops:
  0.6 18.7 %exchange.1 = (f32[64,128]{1,0:T(8,128)S(1)}, f32[1,64]{1,0:T(1,128)S(1)}) custom-call(bf16[128,128]{1,0:T(8,128)(2,1)} %embed_hbm.1, s32[1,128]{1,0:T(1,128)} %bitcast.3, f32[1,128]{1,0:T(1,128)} %bitcast.4), custom_call_target="tpu_custom_call" | custom-call | tf_op jit(solution)/shard_map/exchange/pallas_call | solution.py:293
  19.3 0.6 %write_out.1 = (f32[64,128]{1,0:T(8,128)}, f32[1,64]{1,0:T(1,128)}) custom-call(f32[64,128]{1,0:T(8,128)S(1)} %get-tuple-element.6.mean, f32[1,64]{1,0:T(1,128)S(1)} %get-tuple-element.7.rarity), custom_call_target="tpu_custom_call" | custom-call | tf_op jit(solution)/shard_map/write_out/pallas_call | solution.py:318

commit v5 on v4

--- a/solution.py
+++ b/solution.py
@@ -23,6 +23,11 @@
 REST_LOTS = pl.ds(2 * FIRST, 2 * (DEPTH - FIRST))
 
 
+EARLIEST = 1
+OPPOSITE = 4
+BYPASSED = 129
+
+
 def depth_of(flat):
     return ((flat >> 6) << 1) | ((flat >> 3) & 1)
 
@@ -49,11 +54,17 @@
     return pl.ds(pl.multiple_of(2 * index, 2), 2)
 
 
+def turned_tags(tags_ref):
+    plane = tags_ref[...]
+    totals = jnp.broadcast_to(plane[:, 4 * DEPTH : 4 * DEPTH + 1], (2 * PLANE, 128))
+    return jnp.transpose(jnp.concatenate([plane, totals], axis=0))
+
+
 def exchange(
     embed_hbm, bins_hbm, weights_hbm, mean_ref, rarity_ref,
-    embed, bins, weights, packed, relay, arrived, tags, plane_tags, column, depth_tags,
+    embed, bins, weights, packed, relay, arrived, tags, plane_tags, direct_tags, column, depth_tags,
     in_sems, send_plane, recv_plane, recv_rest, send_depth, recv_depth,
-    send_tags, recv_tags, send_column, recv_column, column_ready,
+    send_tags, recv_tags, send_column, recv_column, send_direct, recv_direct, send_rows, column_ready,
 ):
     me = lax.axis_index(AXIS)
     core = me & 1
@@ -87,6 +98,15 @@
         for turn in range(DEPTH - 1):
             greet(other_relay(turn))
 
+    @pl.when(me == EARLIEST)
+    def _():
+        for place in range(PLANE - 1, -1, -1):
+            target = flat_of_depth(OPPOSITE) | flat_of_chip(place >> 1) | (place & 1)
+            if target != BYPASSED:
+                greet(target)
+
+    is_opposite = (my_depth == OPPOSITE).astype(jnp.int32)
+
     for load in loads:
         load.wait()
 
@@ -135,7 +155,14 @@
             packed.at[chip, REST_LOTS], relay.at[my_place, REST_LOTS], send_plane, recv_rest, target
         ).start()
 
+    def hand_direct():
+        remote(tags.at[two(0)], direct_tags.at[two(my_place)], send_direct, recv_direct, EARLIEST).start()
+        remote(
+            packed.at[0, EARLIEST], arrived.at[OPPOSITE, my_place], send_rows, recv_depth, EARLIEST
+        ).start()
+
     def hand_all():
+        pl.when(my_depth == OPPOSITE)(hand_direct)
         for step in STEPS:
             hand_tags(my_chip ^ step, (me ^ flat_of_chip(step)) | 1)
             hand_first(my_chip ^ step, (me ^ flat_of_chip(step)) | 1, step >> 2)
@@ -145,7 +172,7 @@
 
     @pl.when(core == 0)
     def _():
-        pl.semaphore_wait(barrier, CHIPS)
+        pl.semaphore_wait(barrier, CHIPS + is_opposite)
         hand_all()
         hand_tags(my_chip, me ^ 1)
         hand_first(my_chip, me ^ 1, 0)
@@ -156,7 +183,7 @@
 
     @pl.when(core == 1)
     def _():
-        pl.semaphore_wait(barrier, CHIPS - 1 + DEPTH - 1 + 1)
+        pl.semaphore_wait(barrier, CHIPS - 1 + DEPTH - 1 + 1 + jnp.where(me == BYPASSED, 0, is_opposite))
         hand_all()
         for step in STEPS:
             hand_rest(my_chip ^ step, (me ^ flat_of_chip(step)) | 1)
@@ -170,7 +197,10 @@
             for depth in depths:
                 column_at = bottom | flat_of_depth(depth)
                 send_to(column_at, 2 * depth)
-                pl.when(my_depth != depth)(functools.partial(send_to, column_at | 1, 2 * depth + 1))
+                wanted = my_depth != depth
+                if depth == 0:
+                    wanted = wanted & (me != BYPASSED)
+                pl.when(wanted)(functools.partial(send_to, column_at | 1, 2 * depth + 1))
 
         def pass_on(group):
             count = 8 if group else 7
@@ -190,14 +220,7 @@
 
         others = plane_tags.at[pl.ds(0, 2 * (PLANE - 1))]
         remote(others, others, send_tags, recv_tags, me ^ 1).wait_recv()
-        plane = plane_tags[...]
-        wide_lanes = lax.broadcasted_iota(jnp.int32, (2 * PLANE, 128), 1)
-        wide_rows = lax.broadcasted_iota(jnp.int32, (2 * PLANE, 128), 0)
-        plane_total = jnp.sum(jnp.where(wide_lanes == 4 * DEPTH, plane, 0.0))
-        spare = jnp.where(
-            (wide_lanes < 4 * DEPTH) & (wide_lanes % 2 == 0) & (wide_rows == 0), plane_total, 0.0
-        )
-        column[...] = jnp.transpose(jnp.concatenate([plane, spare], axis=0))[: 4 * DEPTH]
+        column[...] = turned_tags(plane_tags)[: 4 * DEPTH]
 
         def send_column_to(target, lot):
             remote(
@@ -215,18 +238,29 @@
 
         both_cores(range(FIRST, DEPTH), send_rest_to)
         arrived[my_depth] = relay[:, my_depth * 2 + 1]
-        most = depth_tags.at[pl.ds(0, 2 * (DEPTH - 1))]
-        remote(most, most, send_column, recv_column, me ^ 1).wait_recv()
+
+        @pl.when(me != EARLIEST)
+        def _():
+            most = depth_tags.at[pl.ds(0, 2 * (DEPTH - 1))]
+            remote(most, most, send_column, recv_column, me ^ 1).wait_recv()
+
+        @pl.when(me == EARLIEST)
+        def _():
+            remote(direct_tags, direct_tags, send_direct, recv_direct, me ^ 1).wait_recv()
+            turned = turned_tags(direct_tags)
+            most = depth_tags.at[pl.ds(0, 2 * (DEPTH - 2))]
+            remote(most, most, send_column, recv_column, me ^ 1).wait_recv()
+            depth_tags[two(OPPOSITE)] = turned[2 * EARLIEST : 2 * EARLIEST + 2]
 
     half = lax.broadcasted_iota(jnp.int32, (1, 128), 1) < 64
     labels = lax.broadcasted_iota(jnp.int32, (BINS_DEV, 128), 0).astype(jnp.float32)
-    total = jnp.zeros((1, 1), jnp.float32)
+    totals = jnp.zeros((1, 128), jnp.float32)
     weighed = jnp.zeros((BINS_DEV, 128), jnp.float32)
     selectors = []
     for pair in range(DEPTH // 2):
         first = depth_tags[4 * pair : 4 * pair + 2]
         second = depth_tags[4 * pair + 2 : 4 * pair + 4]
-        total = total + first[0:1, 64:65] + second[0:1, 64:65]
+        totals = totals + first[0:1] + second[0:1]
         turned = pltpu.roll(second, 64, axis=1)
         weight = jnp.where(half, first[0:1], turned[0:1])
         offset = jnp.where(half, first[1:2], turned[1:2])
@@ -234,6 +268,7 @@
         weighed = weighed + jnp.where(chosen, weight, 0.0)
         selectors.append(jnp.where(chosen, 1.0, 0.0).astype(jnp.bfloat16))
     den = jnp.broadcast_to(jnp.sum(weighed, axis=1, keepdims=True), (BINS_DEV, 128)) + 1.0
+    total = jnp.sum(jnp.where(half, 0.0, totals), axis=1, keepdims=True)
     rarity_ref[...] = jnp.log(total / (BINS_DEV * DEVICES)) - jnp.log(jnp.transpose(den)[0:1, :BINS_DEV])
 
     @pl.when(core == 0)
@@ -263,10 +298,22 @@
     @pl.when(core == 1)
     def _():
         sent(CHIPS - 1)
-        part = relay.at[pl.ds(0, 2 * (2 * DEPTH - 1))]
+
+    def relayed(targets):
+        part = relay.at[pl.ds(0, 2 * targets)]
         remote(part, part, send_depth, recv_depth, me ^ 1).wait_send()
-        part = column.at[pl.ds(0, 2 * (2 * DEPTH - 1))]
+        part = column.at[pl.ds(0, 2 * targets)]
         remote(part, part, send_column, recv_column, me ^ 1).wait_send()
+
+    pl.when((core == 1) & (me != BYPASSED))(functools.partial(relayed, 2 * DEPTH - 1))
+    pl.when(me == BYPASSED)(functools.partial(relayed, 2 * DEPTH - 2))
+
+    @pl.when(my_depth == OPPOSITE)
+    def _():
+        part = tags.at[two(0)]
+        remote(part, part, send_direct, recv_direct, me ^ 1).wait_send()
+        part = packed.at[0, EARLIEST]
+        remote(part, part, send_rows, recv_depth, me ^ 1).wait_send()
 
 
 def write_out(mean, rarity, mean_hbm, rarity_hbm, sems):
@@ -304,9 +351,11 @@
             pltpu.VMEM((DEPTH, PLANE, 2, width), jnp.bfloat16),
             pltpu.VMEM((2 * CHIPS, 128), jnp.float32),
             pltpu.VMEM((2 * PLANE, 128), jnp.float32),
+            pltpu.VMEM((2 * PLANE, 128), jnp.float32),
             pltpu.VMEM((4 * DEPTH, 128), jnp.float32),
             pltpu.VMEM((2 * DEPTH, 128), jnp.float32),
             dma((3,)), dma(()), dma((4,)), dma(()), dma(()), dma(()), dma(()), dma(()), dma(()), dma(()),
+            dma(()), dma(()), dma(()),
             pltpu.SemaphoreType.REGULAR,
         ],
         compiler_params=pltpu.CompilerParams(collective_id=0, has_side_effects=True, vmem_limit_bytes=4 << 20),

time: 20.1 us -> 19.6 us (0.975)
  Pallas kernels: 19.3 us -> 18.9 us
    pallas_call x1, Pallas kernels: 18.7 us -> 18.2 us  [shards(): pl.pallas_call(exchange, out_shape=shapes, in_specs=[hbm] * 3, out_specs=...]
where the time goes in v5:
time: 19.6 us; the launch traced here: 19.5 us
  Pallas kernels  18.9 us (96%)
  between operations  0.64 us (3%)
    pallas_call x1, Pallas kernels, shards(): pl.pallas_call(exchange, out_shape=shapes, in_specs=[hbm] * 3, out_specs=...  18.2 us
    pallas_call x1, Pallas kernels, shards(): pl.pallas_call(write_out, out_shape=shapes, in_specs=[vmem, vmem], out_sp...  0.64 us

profile of v5, /device:TPU:1, one launch (start us, length us, event | category | flops | bytes accessed | tf_op | source)
XLA Modules:
  0.0 19.5 jit_solution(11796883097966709455)
XLA Ops:
  0.6 18.2 %exchange.1 = (f32[64,128]{1,0:T(8,128)S(1)}, f32[1,64]{1,0:T(1,128)S(1)}) custom-call(bf16[128,128]{1,0:T(8,128)(2,1)} %embed_hbm.1, s32[1,128]{1,0:T(1,128)} %bitcast.3, f32[1,128]{1,0:T(1,128)} %bitcast.4), custom_call_target="tpu_custom_call" | custom-call | tf_op jit(solution)/shard_map/exchange/pallas_call | solution.py:340
  18.9 0.6 %write_out.1 = (f32[64,128]{1,0:T(8,128)}, f32[1,64]{1,0:T(1,128)}) custom-call(f32[64,128]{1,0:T(8,128)S(1)} %get-tuple-element.6.mean, f32[1,64]{1,0:T(1,128)S(1)} %get-tuple-element.7.rarity), custom_call_target="tpu_custom_call" | custom-call | tf_op jit(solution)/shard_map/write_out/pallas_call | solution.py:367

commit v6 on v5

--- a/solution.py
+++ b/solution.py
@@ -18,14 +18,18 @@
 HOPS = (0, 1, 2, 1)
 STEPS = sorted(range(1, CHIPS), key=lambda step: -(HOPS[step >> 2] + HOPS[step & 3]))
 GROUPS = (0, 3, 1, 2)
-FIRST = 1
-FIRST_LOTS = pl.ds(0, 2 * FIRST)
-REST_LOTS = pl.ds(2 * FIRST, 2 * (DEPTH - FIRST))
-
-
+FIRST_LOTS = pl.ds(0, 2)
+TIERS = ((1, 3), (3, 8))
+
+
+def lots_of(tier):
+    return pl.ds(2 * tier[0], 2 * (tier[1] - tier[0]))
+
+
+LATE = 4
 EARLIEST = 1
-OPPOSITE = 4
-BYPASSED = 129
+DIRECT = (4, 5)
+BYPASSED = (129, 137)
 
 
 def depth_of(flat):
@@ -64,7 +68,7 @@
     embed_hbm, bins_hbm, weights_hbm, mean_ref, rarity_ref,
     embed, bins, weights, packed, relay, arrived, tags, plane_tags, direct_tags, column, depth_tags,
     in_sems, send_plane, recv_plane, recv_rest, send_depth, recv_depth,
-    send_tags, recv_tags, send_column, recv_column, send_direct, recv_direct, send_rows, column_ready,
+    send_tags, recv_tags, send_column, recv_column, send_direct, recv_direct, send_rows, above_ready, below_ready,
 ):
     me = lax.axis_index(AXIS)
     core = me & 1
@@ -85,8 +89,12 @@
     def greet(target):
         pl.semaphore_signal(barrier, inc=1, device_id=target, device_id_type=LOGICAL)
 
-    def other_relay(turn):
-        return bottom | flat_of_depth(turn + (turn >= my_depth).astype(jnp.int32)) | 1
+    def relays(first, last, act):
+        def visit(depth, carry):
+            act(bottom | flat_of_depth(depth) | 1)
+            return carry
+
+        lax.fori_loop(first, last, visit, 0)
 
     greet(me ^ 1)
 
@@ -95,17 +103,22 @@
         for step in STEPS:
             greet(me ^ flat_of_chip(step))
             greet(me ^ flat_of_chip(step) ^ 1)
-        for turn in range(DEPTH - 1):
-            greet(other_relay(turn))
+
+    @pl.when((core == 1) | (my_depth < LATE))
+    def _():
+        relays(my_depth + 1, DEPTH, greet)
 
     @pl.when(me == EARLIEST)
     def _():
         for place in range(PLANE - 1, -1, -1):
-            target = flat_of_depth(OPPOSITE) | flat_of_chip(place >> 1) | (place & 1)
-            if target != BYPASSED:
-                greet(target)
-
-    is_opposite = (my_depth == OPPOSITE).astype(jnp.int32)
+            for depth in DIRECT:
+                target = flat_of_depth(depth) | flat_of_chip(place >> 1) | (place & 1)
+                if target not in BYPASSED:
+                    greet(target)
+
+    is_direct = (my_depth == DIRECT[0]) | (my_depth == DIRECT[1])
+    bypassed = (me == BYPASSED[0]) | (me == BYPASSED[1])
+    one_more = is_direct.astype(jnp.int32)
 
     for load in loads:
         load.wait()
@@ -150,19 +163,21 @@
             send_plane, recv_plane.at[group], target,
         ).start()
 
-    def hand_rest(chip, target):
+    def hand_tier(index, chip, target):
+        lots = lots_of(TIERS[index])
         remote(
-            packed.at[chip, REST_LOTS], relay.at[my_place, REST_LOTS], send_plane, recv_rest, target
+            packed.at[chip, lots], relay.at[my_place, lots], send_plane, recv_rest.at[index], target
         ).start()
 
     def hand_direct():
-        remote(tags.at[two(0)], direct_tags.at[two(my_place)], send_direct, recv_direct, EARLIEST).start()
+        row = (my_depth - DIRECT[0]) * PLANE + my_place
+        remote(tags.at[two(0)], direct_tags.at[two(row)], send_direct, recv_direct, EARLIEST).start()
         remote(
-            packed.at[0, EARLIEST], arrived.at[OPPOSITE, my_place], send_rows, recv_depth, EARLIEST
+            packed.at[0, EARLIEST], arrived.at[my_depth, my_place], send_rows, recv_depth, EARLIEST
         ).start()
 
     def hand_all():
-        pl.when(my_depth == OPPOSITE)(hand_direct)
+        pl.when(is_direct)(hand_direct)
         for step in STEPS:
             hand_tags(my_chip ^ step, (me ^ flat_of_chip(step)) | 1)
             hand_first(my_chip ^ step, (me ^ flat_of_chip(step)) | 1, step >> 2)
@@ -172,34 +187,62 @@
 
     @pl.when(core == 0)
     def _():
-        pl.semaphore_wait(barrier, CHIPS + is_opposite)
+        pl.semaphore_wait(barrier, CHIPS + one_more)
         hand_all()
         hand_tags(my_chip, me ^ 1)
         hand_first(my_chip, me ^ 1, 0)
-        for step in STEPS:
-            hand_rest(my_chip ^ step, (me ^ flat_of_chip(step)) | 1)
-        hand_rest(my_chip, me ^ 1)
+        for index in range(len(TIERS)):
+            for step in STEPS:
+                hand_tier(index, my_chip ^ step, (me ^ flat_of_chip(step)) | 1)
+            hand_tier(index, my_chip, me ^ 1)
         remote(depth_tags.at[all_tags], depth_tags.at[all_tags], send_column, recv_column, me ^ 1).wait_recv()
 
     @pl.when(core == 1)
     def _():
-        pl.semaphore_wait(barrier, CHIPS - 1 + DEPTH - 1 + 1 + jnp.where(me == BYPASSED, 0, is_opposite))
+        greeted = my_depth + jnp.minimum(my_depth, LATE) + jnp.where(bypassed, 0, one_more)
+        pl.semaphore_wait(barrier, CHIPS + greeted)
         hand_all()
-        for step in STEPS:
-            hand_rest(my_chip ^ step, (me ^ flat_of_chip(step)) | 1)
-        for turn in range(DEPTH - 1):
-            pl.semaphore_signal(column_ready, inc=1, device_id=other_relay(turn), device_id_type=LOGICAL)
+
+        def answer(target):
+            pl.semaphore_signal(above_ready, inc=1, device_id=target, device_id_type=LOGICAL)
+
+        relays(0, my_depth, answer)
+        for index in range(len(TIERS)):
+            for step in STEPS:
+                hand_tier(index, my_chip ^ step, (me ^ flat_of_chip(step)) | 1)
         relay[my_place] = packed[my_chip]
         plane_tags[two(my_place)] = tags[two(my_chip)]
-        pl.semaphore_wait(column_ready, DEPTH - 1)
-
-        def both_cores(depths, send_to):
+
+        @pl.when((my_depth >= LATE) & (my_depth < DEPTH - 1))
+        def _():
+            pl.semaphore_wait(above_ready, DEPTH - 1 - my_depth)
+
+            def answer_late(target):
+                pl.semaphore_signal(below_ready, inc=1, device_id=target, device_id_type=LOGICAL)
+
+            relays(my_depth + 1, DEPTH, answer_late)
+
+        def await_column():
+            @pl.when(my_depth > LATE)
+            def _():
+                pl.semaphore_wait(below_ready, my_depth - LATE)
+
+            @pl.when(my_depth < LATE)
+            def _():
+                pl.semaphore_wait(above_ready, DEPTH - 1 - my_depth)
+
+        def both_cores(depths, send_to, only=None):
             for depth in depths:
                 column_at = bottom | flat_of_depth(depth)
-                send_to(column_at, 2 * depth)
                 wanted = my_depth != depth
+                if only is None:
+                    send_to(column_at, 2 * depth)
+                else:
+                    chosen = only(depth)
+                    pl.when(chosen)(functools.partial(send_to, column_at, 2 * depth))
+                    wanted = wanted & chosen
                 if depth == 0:
-                    wanted = wanted & (me != BYPASSED)
+                    wanted = wanted & jnp.logical_not(bypassed)
                 pl.when(wanted)(functools.partial(send_to, column_at | 1, 2 * depth + 1))
 
         def pass_on(group):
@@ -213,7 +256,7 @@
                     relay.at[members, lot], arrived.at[my_depth, members], send_depth, recv_depth, target
                 ).start()
 
-            both_cores(range(FIRST), send_to)
+            both_cores(range(1), send_to)
 
         for group in GROUPS[:3]:
             pass_on(group)
@@ -227,16 +270,21 @@
                 column.at[two(lot)], depth_tags.at[two(my_depth)], send_column, recv_column, target
             ).start()
 
-        both_cores(range(DEPTH), send_column_to)
+        both_cores(range(1), send_column_to)
+        both_cores(range(1, LATE), send_column_to, lambda depth: my_depth >= depth)
         depth_tags[two(my_depth)] = column[two(my_depth * 2 + 1)]
         pass_on(GROUPS[3])
-        part = relay.at[pl.ds(0, PLANE - 1), REST_LOTS]
-        remote(part, part, send_plane, recv_rest, me ^ 1).wait_recv()
+        await_column()
+        both_cores(range(1, LATE), send_column_to, lambda depth: my_depth < depth)
+        both_cores(range(LATE, DEPTH), send_column_to)
 
         def send_rest_to(target, lot):
             remote(relay.at[:, lot], arrived.at[my_depth], send_depth, recv_depth, target).start()
 
-        both_cores(range(FIRST, DEPTH), send_rest_to)
+        for index, tier in enumerate(TIERS):
+            part = relay.at[pl.ds(0, PLANE - 1), lots_of(tier)]
+            remote(part, part, send_plane, recv_rest.at[index], me ^ 1).wait_recv()
+            both_cores(range(*tier), send_rest_to)
         arrived[my_depth] = relay[:, my_depth * 2 + 1]
 
         @pl.when(me != EARLIEST)
@@ -247,10 +295,18 @@
         @pl.when(me == EARLIEST)
         def _():
             remote(direct_tags, direct_tags, send_direct, recv_direct, me ^ 1).wait_recv()
-            turned = turned_tags(direct_tags)
-            most = depth_tags.at[pl.ds(0, 2 * (DEPTH - 2))]
+            turned = jnp.transpose(direct_tags[...])
+            pair = turned[2 * EARLIEST : 2 * EARLIEST + 2]
+            totals = jnp.broadcast_to(turned[4 * DEPTH : 4 * DEPTH + 1], (2, 128))
+            lower = lax.broadcasted_iota(jnp.int32, (2, 128), 1) < 64
+            depth_tags[2 * DIRECT[0] : 2 * DIRECT[0] + 2] = jnp.where(
+                lower, pair, pltpu.roll(totals, 64, axis=1)
+            )
+            depth_tags[2 * DIRECT[1] : 2 * DIRECT[1] + 2] = jnp.where(
+                lower, pltpu.roll(pair, 64, axis=1), totals
+            )
+            most = depth_tags.at[pl.ds(0, 2 * (DEPTH - 1 - len(DIRECT)))]
             remote(most, most, send_column, recv_column, me ^ 1).wait_recv()
-            depth_tags[two(OPPOSITE)] = turned[2 * EARLIEST : 2 * EARLIEST + 2]
 
     half = lax.broadcasted_iota(jnp.int32, (1, 128), 1) < 64
     labels = lax.broadcasted_iota(jnp.int32, (BINS_DEV, 128), 0).astype(jnp.float32)
@@ -267,18 +323,18 @@
         chosen = labels == offset
         weighed = weighed + jnp.where(chosen, weight, 0.0)
         selectors.append(jnp.where(chosen, 1.0, 0.0).astype(jnp.bfloat16))
+    @pl.when(core == 0)
+    def _():
+        remote(everything, everything, send_depth, recv_depth, me ^ 1).wait_recv()
+
+    @pl.when(core == 1)
+    def _():
+        most = arrived.at[pl.ds(0, DEPTH - 1)]
+        remote(most, most, send_depth, recv_depth, me ^ 1).wait_recv()
+
     den = jnp.broadcast_to(jnp.sum(weighed, axis=1, keepdims=True), (BINS_DEV, 128)) + 1.0
     total = jnp.sum(jnp.where(half, 0.0, totals), axis=1, keepdims=True)
     rarity_ref[...] = jnp.log(total / (BINS_DEV * DEVICES)) - jnp.log(jnp.transpose(den)[0:1, :BINS_DEV])
-
-    @pl.when(core == 0)
-    def _():
-        remote(everything, everything, send_depth, recv_depth, me ^ 1).wait_recv()
-
-    @pl.when(core == 1)
-    def _():
-        most = arrived.at[pl.ds(0, DEPTH - 1)]
-        remote(most, most, send_depth, recv_depth, me ^ 1).wait_recv()
 
     mean_ref[...] = jnp.dot(
         jnp.concatenate(selectors, axis=1), arrived.reshape(2 * DEVICES, 128)[...],
@@ -305,10 +361,10 @@
         part = column.at[pl.ds(0, 2 * targets)]
         remote(part, part, send_column, recv_column, me ^ 1).wait_send()
 
-    pl.when((core == 1) & (me != BYPASSED))(functools.partial(relayed, 2 * DEPTH - 1))
-    pl.when(me == BYPASSED)(functools.partial(relayed, 2 * DEPTH - 2))
-
-    @pl.when(my_depth == OPPOSITE)
+    pl.when((core == 1) & jnp.logical_not(bypassed))(functools.partial(relayed, 2 * DEPTH - 1))
+    pl.when(bypassed)(functools.partial(relayed, 2 * DEPTH - 2))
+
+    @pl.when(is_direct)
     def _():
         part = tags.at[two(0)]
         remote(part, part, send_direct, recv_direct, me ^ 1).wait_send()
@@ -351,12 +407,12 @@
             pltpu.VMEM((DEPTH, PLANE, 2, width), jnp.bfloat16),
             pltpu.VMEM((2 * CHIPS, 128), jnp.float32),
             pltpu.VMEM((2 * PLANE, 128), jnp.float32),
-            pltpu.VMEM((2 * PLANE, 128), jnp.float32),
+            pltpu.VMEM((2 * len(DIRECT) * PLANE, 128), jnp.float32),
             pltpu.VMEM((4 * DEPTH, 128), jnp.float32),
             pltpu.VMEM((2 * DEPTH, 128), jnp.float32),
-            dma((3,)), dma(()), dma((4,)), dma(()), dma(()), dma(()), dma(()), dma(()), dma(()), dma(()),
+            dma((3,)), dma(()), dma((4,)), dma((len(TIERS),)), dma(()), dma(()), dma(()), dma(()), dma(()), dma(()),
             dma(()), dma(()), dma(()),
-            pltpu.SemaphoreType.REGULAR,
+            pltpu.SemaphoreType.REGULAR, pltpu.SemaphoreType.REGULAR,
         ],
         compiler_params=pltpu.CompilerParams(collective_id=0, has_side_effects=True, vmem_limit_bytes=4 << 20),
         name="exchange",

time: 19.6 us -> 19.1 us (0.974)
  Pallas kernels: 18.9 us -> 18.3 us
    pallas_call x1, Pallas kernels: 18.2 us -> 17.6 us  [shards(): pl.pallas_call(exchange, out_shape=shapes, in_specs=[hbm] * 3, out_specs=...]
where the time goes in v6:
time: 19.1 us; the launch traced here: 18.9 us
  Pallas kernels  18.3 us (96%)
  between operations  0.64 us (3%)
    pallas_call x1, Pallas kernels, shards(): pl.pallas_call(exchange, out_shape=shapes, in_specs=[hbm] * 3, out_specs=...  17.6 us
    pallas_call x1, Pallas kernels, shards(): pl.pallas_call(write_out, out_shape=shapes, in_specs=[vmem, vmem], out_sp...  0.64 us

profile of v6, /device:TPU:1, one launch (start us, length us, event | category | flops | bytes accessed | tf_op | source)
XLA Modules:
  0.0 18.9 jit_solution(10528861500903202290)
XLA Ops:
  0.6 17.6 %exchange.1 = (f32[64,128]{1,0:T(8,128)S(1)}, f32[1,64]{1,0:T(1,128)S(1)}) custom-call(bf16[128,128]{1,0:T(8,128)(2,1)} %embed_hbm.1, s32[1,128]{1,0:T(1,128)} %bitcast.3, f32[1,128]{1,0:T(1,128)} %bitcast.4), custom_call_target="tpu_custom_call" | custom-call | tf_op jit(solution)/shard_map/exchange/pallas_call | solution.py:396
  18.3 0.6 %write_out.1 = (f32[64,128]{1,0:T(8,128)}, f32[1,64]{1,0:T(1,128)}) custom-call(f32[64,128]{1,0:T(8,128)S(1)} %get-tuple-element.6.mean, f32[1,64]{1,0:T(1,128)S(1)} %get-tuple-element.7.rarity), custom_call_target="tpu_custom_call" | custom-call | tf_op jit(solution)/shard_map/write_out/pallas_call | solution.py:423

commit v7 on v6

--- a/solution.py
+++ b/solution.py
@@ -28,8 +28,8 @@
 
 LATE = 4
 EARLIEST = 1
-DIRECT = (4, 5)
-BYPASSED = (129, 137)
+DIRECT = (4, 5, 6)
+BYPASSED = (129, 137, 193)
 
 
 def depth_of(flat):
@@ -116,8 +116,8 @@
                 if target not in BYPASSED:
                     greet(target)
 
-    is_direct = (my_depth == DIRECT[0]) | (my_depth == DIRECT[1])
-    bypassed = (me == BYPASSED[0]) | (me == BYPASSED[1])
+    is_direct = (my_depth >= DIRECT[0]) & (my_depth <= DIRECT[-1])
+    bypassed = is_direct & (my_chip == 0) & (core == 1)
     one_more = is_direct.astype(jnp.int32)
 
     for load in loads:
@@ -235,15 +235,16 @@
             for depth in depths:
                 column_at = bottom | flat_of_depth(depth)
                 wanted = my_depth != depth
-                if only is None:
-                    send_to(column_at, 2 * depth)
-                else:
-                    chosen = only(depth)
-                    pl.when(chosen)(functools.partial(send_to, column_at, 2 * depth))
+                chosen = True if only is None else only(depth)
+                if only is not None:
                     wanted = wanted & chosen
                 if depth == 0:
                     wanted = wanted & jnp.logical_not(bypassed)
                 pl.when(wanted)(functools.partial(send_to, column_at | 1, 2 * depth + 1))
+                if only is None:
+                    send_to(column_at, 2 * depth)
+                else:
+                    pl.when(chosen)(functools.partial(send_to, column_at, 2 * depth))
 
         def pass_on(group):
             count = 8 if group else 7
@@ -270,21 +271,28 @@
                 column.at[two(lot)], depth_tags.at[two(my_depth)], send_column, recv_column, target
             ).start()
 
+        def known(depth):
+            return my_depth >= depth
+
+        def unknown(depth):
+            return my_depth < depth
+
         both_cores(range(1), send_column_to)
-        both_cores(range(1, LATE), send_column_to, lambda depth: my_depth >= depth)
+        both_cores(range(1, LATE), send_column_to, known)
         depth_tags[two(my_depth)] = column[two(my_depth * 2 + 1)]
         pass_on(GROUPS[3])
-        await_column()
-        both_cores(range(1, LATE), send_column_to, lambda depth: my_depth < depth)
-        both_cores(range(LATE, DEPTH), send_column_to)
-
         def send_rest_to(target, lot):
             remote(relay.at[:, lot], arrived.at[my_depth], send_depth, recv_depth, target).start()
 
         for index, tier in enumerate(TIERS):
             part = relay.at[pl.ds(0, PLANE - 1), lots_of(tier)]
             remote(part, part, send_plane, recv_rest.at[index], me ^ 1).wait_recv()
-            both_cores(range(*tier), send_rest_to)
+            both_cores(range(tier[0], min(tier[1], LATE)), send_rest_to, known)
+        await_column()
+        both_cores(range(1, LATE), send_column_to, unknown)
+        both_cores(range(LATE, DEPTH), send_column_to)
+        both_cores(range(1, LATE), send_rest_to, unknown)
+        both_cores(range(LATE, DEPTH), send_rest_to)
         arrived[my_depth] = relay[:, my_depth * 2 + 1]
 
         @pl.when(me != EARLIEST)
@@ -295,7 +303,7 @@
         @pl.when(me == EARLIEST)
         def _():
             remote(direct_tags, direct_tags, send_direct, recv_direct, me ^ 1).wait_recv()
-            turned = jnp.transpose(direct_tags[...])
+            turned = jnp.transpose(direct_tags[: 4 * PLANE])
             pair = turned[2 * EARLIEST : 2 * EARLIEST + 2]
             totals = jnp.broadcast_to(turned[4 * DEPTH : 4 * DEPTH + 1], (2, 128))
             lower = lax.broadcasted_iota(jnp.int32, (2, 128), 1) < 64
@@ -305,6 +313,8 @@
             depth_tags[2 * DIRECT[1] : 2 * DIRECT[1] + 2] = jnp.where(
                 lower, pltpu.roll(pair, 64, axis=1), totals
             )
+            turned = turned_tags(direct_tags.at[pl.ds(4 * PLANE, 2 * PLANE)])
+            depth_tags[2 * DIRECT[2] : 2 * DIRECT[2] + 2] = turned[2 * EARLIEST : 2 * EARLIEST + 2]
             most = depth_tags.at[pl.ds(0, 2 * (DEPTH - 1 - len(DIRECT)))]
             remote(most, most, send_column, recv_column, me ^ 1).wait_recv()
 

time: 19.1 us -> 18.7 us (0.979)
  Pallas kernels: 18.3 us -> 17.8 us
    pallas_call x1, Pallas kernels: 17.6 us -> 17.1 us  [shards(): pl.pallas_call(exchange, out_shape=shapes, in_specs=[hbm] * 3, out_specs=...]
where the time goes in v7:
time: 18.7 us; the launch traced here: 18.4 us
  Pallas kernels  17.8 us (95%)
  between operations  0.64 us (3%)
    pallas_call x1, Pallas kernels, shards(): pl.pallas_call(exchange, out_shape=shapes, in_specs=[hbm] * 3, out_specs=...  17.1 us
    pallas_call x1, Pallas kernels, shards(): pl.pallas_call(write_out, out_shape=shapes, in_specs=[vmem, vmem], out_sp...  0.64 us

profile of v7, /device:TPU:1, one launch (start us, length us, event | category | flops | bytes accessed | tf_op | source)
XLA Modules:
  0.0 18.4 jit_solution(7870332908253319004)
XLA Ops:
  0.6 17.1 %exchange.1 = (f32[64,128]{1,0:T(8,128)S(1)}, f32[1,64]{1,0:T(1,128)S(1)}) custom-call(bf16[128,128]{1,0:T(8,128)(2,1)} %embed_hbm.1, s32[1,128]{1,0:T(1,128)} %bitcast.3, f32[1,128]{1,0:T(1,128)} %bitcast.4), custom_call_target="tpu_custom_call" | custom-call | tf_op jit(solution)/shard_map/exchange/pallas_call | solution.py:406
  17.8 0.6 %write_out.1 = (f32[64,128]{1,0:T(8,128)}, f32[1,64]{1,0:T(1,128)}) custom-call(f32[64,128]{1,0:T(8,128)S(1)} %get-tuple-element.6.mean, f32[1,64]{1,0:T(1,128)S(1)} %get-tuple-element.7.rarity), custom_call_target="tpu_custom_call" | custom-call | tf_op jit(solution)/shard_map/write_out/pallas_call | solution.py:433

commit v8 on v7

--- a/solution.py
+++ b/solution.py
@@ -235,16 +235,22 @@
             for depth in depths:
                 column_at = bottom | flat_of_depth(depth)
                 wanted = my_depth != depth
-                chosen = True if only is None else only(depth)
-                if only is not None:
+                chosen = None if only is None else only(depth)
+                if chosen is not None:
                     wanted = wanted & chosen
                 if depth == 0:
                     wanted = wanted & jnp.logical_not(bypassed)
-                pl.when(wanted)(functools.partial(send_to, column_at | 1, 2 * depth + 1))
-                if only is None:
-                    send_to(column_at, 2 * depth)
-                else:
-                    pl.when(chosen)(functools.partial(send_to, column_at, 2 * depth))
+
+                def serve(core, depth=depth, column_at=column_at, wanted=wanted, chosen=chosen):
+                    act = functools.partial(send_to, column_at | core, 2 * depth + core)
+                    condition = wanted if core else chosen
+                    if condition is None:
+                        act()
+                    else:
+                        pl.when(condition)(act)
+
+                for core in (1, 0) if depth == 0 else (0, 1):
+                    serve(core)
 
         def pass_on(group):
             count = 8 if group else 7

time: 18.7 us -> 18.7 us (level)
  no operation moved by 1% of the time
where the time goes in v8:
time: 18.7 us; the launch traced here: 18.4 us
  Pallas kernels  17.8 us (95%)
  between operations  0.64 us (3%)
    pallas_call x1, Pallas kernels, shards(): pl.pallas_call(exchange, out_shape=shapes, in_specs=[hbm] * 3, out_specs=...  17.1 us
    pallas_call x1, Pallas kernels, shards(): pl.pallas_call(write_out, out_shape=shapes, in_specs=[vmem, vmem], out_sp...  0.64 us

profile of v8, /device:TPU:1, one launch (start us, length us, event | category | flops | bytes accessed | tf_op | source)
XLA Modules:
  0.0 18.4 jit_solution(15886238563408958283)
XLA Ops:
  0.6 17.1 %exchange.1 = (f32[64,128]{1,0:T(8,128)S(1)}, f32[1,64]{1,0:T(1,128)S(1)}) custom-call(bf16[128,128]{1,0:T(8,128)(2,1)} %embed_hbm.1, s32[1,128]{1,0:T(1,128)} %bitcast.3, f32[1,128]{1,0:T(1,128)} %bitcast.4), custom_call_target="tpu_custom_call" | custom-call | tf_op jit(solution)/shard_map/exchange/pallas_call | solution.py:412
  17.8 0.6 %write_out.1 = (f32[64,128]{1,0:T(8,128)}, f32[1,64]{1,0:T(1,128)}) custom-call(f32[64,128]{1,0:T(8,128)S(1)} %get-tuple-element.6.mean, f32[1,64]{1,0:T(1,128)S(1)} %get-tuple-element.7.rarity), custom_call_target="tpu_custom_call" | custom-call | tf_op jit(solution)/shard_map/write_out/pallas_call | solution.py:439
